TPU v7x, 256 devices: a whole 4x4x8 slice. The times are simulated.
256 devices in a mesh: row: 2 (over core), col: 4 (over x), depth: 32 (over z, y).
Axes of the slice: x: 4, y: 4, z: 8, core: 2. Of those that a mesh axis runs over, the one named last changes fastest.
Arguments:
- a_tile: float32 [2048, 2048], P('row', 'col'), as said below
- panels: float32 [2048, 32768], P('row', 'depth'), as said below
Outputs:
- trailing: float32 [2048, 2048], P(('row', 'depth'), 'col')
- new_panel: float32 [2048, 512], P(('row', 'col'))
- diag_norm: float32 [1], replicated
Inputs may be any that keep to these rules, and one draw needn't show every extreme that they name: symmetric; a_tile - panels panels^T is positive definite with a large positive diagonal. `panels`: real-valued entries of full rank.
All inputs are finite; a program needn't handle non-finite values.
Results may differ from a plain program's by a relative error of at most 0.00015.
Values sent between devices are 32-bit elements; how exact they have to be, the bound alone decides.
No kernel may reach another device: no remote copies, remote signals or barrier semaphores. Data moves between devices by JAX's collectives and lax.ppermute only.
A program may use at most 64 MiB of HBM per device.

v0:
```python
import jax
import jax.numpy as jnp
from jax import lax
from jax.experimental import pallas as pl
from jax.experimental.pallas import tpu as pltpu
from jax.sharding import Mesh
from jax.sharding import PartitionSpec as P


PB = 512
LANES = 128
SUBLANES = 8
GROUPS = LANES // SUBLANES
TILE = (SUBLANES, LANES)
BLOCKS = PB // LANES
PAIRS = BLOCKS * (BLOCKS + 1) // 2
DEPTH = ("depth_0", "depth_1")
ROW_DEPTH = ("row", "depth_0", "depth_1")
Z, Y = DEPTH
Y_SIZE = 4
WIDE = PB // LANES
SLOTS = 3
SUM_PIECE, SUM_SLOT = divmod(PAIRS * GROUPS // 2, SLOTS)
HALVES = (((0, 0), (3, 0), (3, 1), (3, 2), (3, 3)), ((1, 0), (1, 1), (2, 0), (2, 1), (2, 2)))
F32 = jnp.float32


def times_transposed(left, right):
    return lax.dot_general(
        left,
        right,
        (((1,), (1,)), ((), ())),
        precision=lax.Precision.HIGHEST,
        preferred_element_type=F32,
    )


def pair(i, j):
    return i * (i + 1) // 2 + j


def inverse_factor(load, store):
    lane = lax.broadcasted_iota(jnp.int32, (SUBLANES, LANES), 1)
    sub = lax.broadcasted_iota(jnp.int32, (SUBLANES, LANES), 0)
    whole = (SUBLANES, LANES)
    rows = [load(h) for h in range(GROUPS)]
    for g in range(GROUPS):
        first = SUBLANES * g
        cols = {
            h: [
                jnp.broadcast_to(rows[h][:, first + j : first + j + 1], whole)
                for j in range(SUBLANES)
            ]
            for h in range(g, GROUPS)
        }
        inside = (lane >= first) & (lane < first + SUBLANES)
        rows[g] = jnp.where(inside, jnp.where(lane - first == sub, 1.0, 0.0), rows[g])
        for h in range(g + 1, GROUPS):
            rows[h] = jnp.where(inside, 0.0, rows[h])
        done = jnp.zeros(whole, F32)
        for j in range(SUBLANES):
            scale = lax.rsqrt(jnp.broadcast_to(cols[g][j][j : j + 1], whole))
            row = jnp.broadcast_to(rows[g][j : j + 1], whole) * scale
            done = jnp.where(sub == j, row, done)
            own = cols[g][j] * scale
            spread = {
                k: jnp.broadcast_to(own[k : k + 1], whole) for k in range(j + 1, SUBLANES)
            }
            for k in spread:
                cols[g][k] = cols[g][k] - own * spread[k]
            rows[g] = rows[g] - jnp.where(sub > j, own, 0.0) * row
            for h in range(g + 1, GROUPS):
                below = cols[h][j] * scale
                rows[h] = rows[h] - below * row
                for k in spread:
                    cols[h][k] = cols[h][k] - below * spread[k]
        store(g, jnp.where(lane <= first + sub, done, 0.0))


def halves(value):
    high = value.astype(jnp.bfloat16)
    return high, (value - high.astype(F32)).astype(jnp.bfloat16)


def product(left, right):
    def dot(a, b):
        return lax.dot_general(a, b, (((1,), (1,)), ((), ())), preferred_element_type=F32)

    return dot(left[0], right[0]) + (dot(left[0], right[1]) + dot(left[1], right[0]))


def top_kernel(place_ref, near_ref, top_in_ref, out_ref, own_ref, top_ref, all_ref, sem):
    r, c = place_ref[0], place_ref[1]
    count = own_ref.shape[0]
    first = pl.multiple_of(c * count, count)
    own = pltpu.make_async_copy(near_ref.at[pl.ds(first, count)], own_ref, sem.at[0])
    every = pltpu.make_async_copy(near_ref, all_ref, sem.at[2])
    own.start()

    @pl.when(r == 0)
    def _():
        pltpu.make_async_copy(near_ref.at[pl.ds(0, PB)], top_ref, sem.at[1]).start()

    @pl.when(r != 0)
    def _():
        pltpu.make_async_copy(top_in_ref, top_ref, sem.at[1]).start()

    every.start()
    own.wait()
    pltpu.make_async_copy(top_in_ref, top_ref, sem.at[1]).wait()
    right = halves(top_ref[...])
    value = product(halves(own_ref[...]), right)
    for d in range(32):
        for l in range(WIDE):
            out_ref[d, SLOTS + l] = value[
                SUBLANES * d : SUBLANES * (d + 1), LANES * l : LANES * (l + 1)
            ]
    for half in range(2):

        @pl.when(r == half)
        def _(half=half):
            levels = sorted({i for i, _ in HALVES[half]})
            left = tuple(
                jnp.concatenate([x[LANES * i : LANES * (i + 1)] for i in levels]) for x in right
            )
            value = product(left, right)
            for b, (i, j) in enumerate(HALVES[half]):
                for h in range(GROUPS):
                    d, k = divmod(b * GROUPS + h, SLOTS)
                    row = LANES * levels.index(i) + SUBLANES * h
                    out_ref[d, k] = value[row : row + SUBLANES, LANES * j : LANES * (j + 1)]

    for t in range(PAIRS * GROUPS // 2 + 1, 32 * SLOTS):
        out_ref[t // SLOTS, t % SLOTS] = jnp.zeros(TILE, F32)
    every.wait()
    folded = jnp.zeros((all_ref.shape[0], LANES), F32)
    for l in range(all_ref.shape[1] // LANES):
        part = all_ref[:, LANES * l : LANES * (l + 1)]
        folded = folded + part * part
    ones = jnp.ones((SUBLANES, LANES), jnp.bfloat16)
    high, low = halves(folded)

    def row_sums(part):
        return lax.dot_general(ones, part, (((1,), (1,)), ((), ())), preferred_element_type=F32)

    sums = row_sums(high) + row_sums(low)
    sub = lax.broadcasted_iota(jnp.int32, TILE, 0)
    tile = jnp.zeros(TILE, F32)
    for a in range(SUBLANES):
        tile = jnp.where(sub == a, sums[:, LANES * a : LANES * (a + 1)], tile)
    out_ref[SUM_PIECE, SUM_SLOT] = tile


def a_kernel(place_ref, a_ref, *refs):
    cols = 4
    outs = refs[:cols]
    tile_buf, panel_buf, own_buf, sem = refs[cols:]
    r, c, d = place_ref[0], place_ref[1], place_ref[2] * Y_SIZE + place_ref[3]
    copies = []
    for k in range(SLOTS):
        t = jnp.minimum(d * SLOTS + k, PAIRS * GROUPS // 2 - 1)
        b, h = t // GROUPS, lax.rem(t, GROUPS)
        places = (
            (jnp.where(b == 0, 0, 3), jnp.where(b == 0, 0, b - 1)),
            (jnp.where(b < 2, 1, 2), jnp.where(b < 2, b, b - 2)),
        )
        for half, (i, j) in enumerate(places):
            row = pl.multiple_of(i * LANES + h * SUBLANES, SUBLANES)
            col = pl.multiple_of(j * LANES, LANES)
            copies.append(
                (a_ref.at[pl.ds(row, SUBLANES), pl.ds(col, LANES)], tile_buf.at[half * SLOTS + k])
            )
    for s in range(cols):
        row = pl.multiple_of(lax.rem(c + s, cols) * 256 + d * SUBLANES, SUBLANES)
        copies.append((a_ref.at[pl.ds(row, SUBLANES), :], panel_buf.at[s]))
    for b in range(BLOCKS):
        row = pl.multiple_of(lax.rem(c, 2) * PB + b * LANES, LANES)
        copies.append((a_ref.at[pl.ds(row, LANES), pl.ds(b * LANES, LANES)], own_buf.at[b]))
    copies = [pltpu.make_async_copy(a, b, sem.at[n]) for n, (a, b) in enumerate(copies)]
    for copy in copies:
        copy.start()
    for copy in copies:
        copy.wait()
    lane = lax.broadcasted_iota(jnp.int32, (LANES, LANES), 1)
    sub = lax.broadcasted_iota(jnp.int32, (LANES, LANES), 0)
    level = lax.broadcasted_iota(jnp.int32, TILE, 0)
    diagonal = jnp.zeros(TILE, F32)
    for b in range(BLOCKS):
        values = jnp.sum(jnp.where(lane == sub, own_buf[b], 0.0), axis=0, keepdims=True)
        here = (level == lax.rem(c, 2) * BLOCKS + b) & (c // 2 == r)
        diagonal = jnp.where(here, jnp.broadcast_to(values, TILE), diagonal)
    root = c == 0
    for s in range(cols):
        for k in range(2 * SLOTS):
            outs[s][k] = jnp.where(root, tile_buf[k], 0.0)
        for l in range(WIDE):
            outs[s][2 * SLOTS + l] = jnp.where(
                root, panel_buf[s, :, LANES * l : LANES * (l + 1)], 0.0
            )
        outs[s][2 * SLOTS + WIDE] = diagonal


def merge_kernel(place_ref, got_ref, a_ref, other_ref, out_ref):
    r, d = place_ref[0], place_ref[2] * Y_SIZE + place_ref[3]
    total = got_ref[0]
    for n in range(1, got_ref.shape[0]):
        total = total + got_ref[n]
    tiles = []
    for k in range(SLOTS):
        a = jnp.where(r == 0, a_ref[k], other_ref[k])
        if k == SUM_SLOT:
            special = d == SUM_PIECE
            value = jnp.where(special, a_ref[2 * SLOTS + WIDE], a) - total[k]
            squares = jnp.sum(jnp.sum(value * value, axis=1, keepdims=True), axis=0, keepdims=True)
            tiles.append(jnp.where(special, jnp.broadcast_to(squares, TILE), value))
        else:
            tiles.append(a - total[k])
    for l in range(WIDE):
        tiles.append(a_ref[2 * SLOTS + l] - total[SLOTS + l])
    for n in range(out_ref.shape[0]):
        for k, tile in enumerate(tiles):
            out_ref[n, k] = tile


def block_kernel(place_ref, left_ref, near_ref, far_ref, *refs):
    outs, high_ref, low_ref, right_ref, sem = refs[:Y_SIZE], *refs[Y_SIZE:]
    r, c, y = place_ref[0], place_ref[1], place_ref[3]
    step = pl.program_id(0)
    here = c // 2 == r
    half = pl.multiple_of(lax.rem(c, 2) * PB, PB)

    @pl.when(step == 0)
    def _():
        @pl.when(here)
        def _():
            pltpu.make_async_copy(near_ref.at[pl.ds(half, PB)], right_ref, sem).start()

        @pl.when(jnp.logical_not(here))
        def _():
            pltpu.make_async_copy(far_ref.at[pl.ds(half, PB)], right_ref, sem).start()

        pltpu.make_async_copy(near_ref.at[pl.ds(half, PB)], right_ref, sem).wait()
        high, low = halves(right_ref[...])
        high_ref[...] = high
        low_ref[...] = low

    value = product(halves(left_ref[...]), (high_ref[...], low_ref[...]))
    for yy in range(Y_SIZE):
        for s in range(Y_SIZE):

            @pl.when(lax.rem(yy - y + Y_SIZE, Y_SIZE) == s)
            def _(yy=yy, s=s):
                for zz in range(outs[s].shape[0]):
                    for g in range(4):
                        for l in range(WIDE):
                            row = LANES * zz + 32 * yy + SUBLANES * g
                            outs[s][zz, g * WIDE + l] = value[
                                row : row + SUBLANES, LANES * l : LANES * (l + 1)
                            ]


def at(i, j):
    return slice(LANES * pair(i, j), LANES * (pair(i, j) + 1))


def block(i):
    return slice(LANES * i, LANES * (i + 1))


def solve_kernel(place_ref, mine_ref, other_ref, x_ref, norm_ref, w, inv_ref):
    r = place_ref[0]
    for half in range(2):
        for ref, take in ((mine_ref, r == half), (other_ref, r != half)):

            @pl.when(take)
            def _(half=half, ref=ref):
                for b, (i, j) in enumerate(HALVES[half]):
                    for h in range(GROUPS):
                        d, k = divmod(b * GROUPS + h, SLOTS)
                        row = LANES * pair(i, j) + SUBLANES * h
                        w[row : row + SUBLANES] = ref[d, k]

    for d in range(mine_ref.shape[0]):
        for l in range(WIDE):
            x_ref[SUBLANES * d : SUBLANES * (d + 1), block(l)] = mine_ref[d, SLOTS + l]
    total = mine_ref[SUM_PIECE, SUM_SLOT] + other_ref[SUM_PIECE, SUM_SLOT]
    norm_ref[...] = jnp.sqrt(total / 2048.0)

    def step(b, carry):
        start = (b * (b + 3)) // 2 * LANES

        def load(h):
            return w[pl.ds(pl.multiple_of(start + SUBLANES * h, SUBLANES), SUBLANES)]

        def store(h, value):
            inv_ref[SUBLANES * h : SUBLANES * (h + 1)] = value

        inverse_factor(load, store)
        for s in range(BLOCKS):

            @pl.when(b == s)
            def _(s=s):
                inv = inv_ref[...]
                for i in range(s + 1, BLOCKS):
                    w[at(i, s)] = times_transposed(w[at(i, s)], inv)
                for j in range(s + 1, BLOCKS):
                    for i in range(j, BLOCKS):
                        w[at(i, j)] = w[at(i, j)] - times_transposed(w[at(i, s)], w[at(j, s)])
                x = times_transposed(x_ref[:, block(s)], inv)
                x_ref[:, block(s)] = x
                for j in range(s + 1, BLOCKS):
                    x_ref[:, block(j)] = x_ref[:, block(j)] - times_transposed(x, w[at(j, s)])

        return carry

    lax.fori_loop(0, BLOCKS, step, 0)


SMEM = pl.BlockSpec(memory_space=pltpu.SMEM)
VMEM = pl.BlockSpec(memory_space=pltpu.VMEM)
ANY = pl.BlockSpec(memory_space=pl.ANY)


def shaped(*dims):
    return jax.ShapeDtypeStruct(dims, F32)


def call(kernel, flops, outs, in_specs, scratch=(), grid=(), out_spec=None):
    out_specs = [out_spec or VMEM] * len(outs)
    return pl.pallas_call(
        kernel,
        out_shape=outs,
        grid=grid,
        in_specs=in_specs,
        out_specs=out_specs,
        scratch_shapes=scratch,
        cost_estimate=pl.CostEstimate(flops=flops, bytes_accessed=4_000_000, transcendentals=0),
    )


def exchange(pieces, axis):
    return lax.all_to_all(pieces, axis, split_axis=0, concat_axis=0, tiled=True)


def shifted(value, axis, by):
    size = lax.axis_size(axis)
    return lax.ppermute(value, axis, [(i, (i + by) % size) for i in range(size)])


def delivered(pieces, axis):
    return [pieces[0]] + [shifted(pieces[s], axis, s) for s in range(1, len(pieces))]


def body(a_tile, panels):
    tile_rows, tile_cols = a_tile.shape
    z_size, depth = lax.axis_size(Z), lax.axis_size(DEPTH)
    c_rows = tile_rows // 4
    share = tile_rows // depth
    k_size = panels.shape[1]
    r, c, d = lax.axis_index("row"), lax.axis_index("col"), lax.axis_index(DEPTH)
    place = jnp.stack([r, c, lax.axis_index(Z), lax.axis_index(Y)]).astype(jnp.int32)
    swap = [(0, 1), (1, 0)]

    top = lax.ppermute(panels[:PB], "row", [(0, 1)])
    far = lax.ppermute(panels, "row", swap)

    piece = shaped(depth, SLOTS + WIDE, *TILE)
    (part,) = call(
        top_kernel,
        8_000_000_000,
        [piece],
        [SMEM, ANY, ANY],
        [
            pltpu.VMEM((c_rows, k_size), F32),
            pltpu.VMEM((PB, k_size), F32),
            pltpu.VMEM((tile_rows, k_size), F32),
            pltpu.SemaphoreType.DMA((3,)),
        ],
    )(place, panels, top)
    got = exchange(part, DEPTH)

    a_sent = call(
        a_kernel,
        1_000_000_000,
        [shaped(2 * SLOTS + WIDE + 1, *TILE)] * 4,
        [SMEM, ANY],
        [
            pltpu.VMEM((2 * SLOTS, *TILE), F32),
            pltpu.VMEM((4, SUBLANES, PB), F32),
            pltpu.VMEM((BLOCKS, LANES, LANES), F32),
            pltpu.SemaphoreType.DMA((2 * SLOTS + 4 + BLOCKS,)),
        ],
    )(place, a_tile)
    a_got = delivered(a_sent, "col")
    a_got = sum(a_got)
    a_other = lax.ppermute(a_got[SLOTS : 2 * SLOTS], "row", [(0, 1)])

    (piece_copies,) = call(
        merge_kernel, 1_000_000_000, [piece], [SMEM, VMEM, VMEM, VMEM]
    )(place, got, a_got, a_other)
    mine = exchange(piece_copies, DEPTH)
    other = lax.ppermute(mine[:, :SLOTS], "row", swap)

    piece = shaped(z_size, 4 * WIDE, *TILE)
    parts = call(
        block_kernel,
        20_000_000_000,
        [piece] * Y_SIZE,
        [SMEM, pl.BlockSpec((PB, k_size), lambda i: (i, 0)), ANY, ANY],
        [
            pltpu.VMEM((PB, k_size), jnp.bfloat16),
            pltpu.VMEM((PB, k_size), jnp.bfloat16),
            pltpu.VMEM((PB, k_size), F32),
            pltpu.SemaphoreType.DMA,
        ],
        grid=(2,),
        out_spec=pl.BlockSpec((z_size // 2, *piece.shape[1:]), lambda i: (i, 0, 0, 0)),
    )(place, panels, panels, far)
    parts = delivered(parts, Y)
    part = sum(parts)
    got = exchange(part, Z)
    tiles = got.sum(axis=0)
    tiles = tiles.reshape(4, WIDE, *TILE).transpose(0, 2, 1, 3).reshape(share, tile_cols)
    trailing = lax.dynamic_slice_in_dim(a_tile, d * share, share, 0) - tiles

    new_panel, norm = call(
        solve_kernel,
        30_000_000_000,
        [shaped(c_rows, PB), shaped(*TILE)],
        [SMEM, VMEM, VMEM],
        [pltpu.VMEM((PAIRS * LANES, LANES), F32), pltpu.VMEM((LANES, LANES), F32)],
    )(place, mine, other)
    return (trailing, new_panel, norm[0, :1])


def solution(mesh):
    finer = Mesh(
        mesh.devices.reshape(mesh.shape["row"], mesh.shape["col"], 8, 4),
        ("row", "col", "depth_0", "depth_1"),
    )
    in_specs = (P("row", "col"), P("row", DEPTH))
    out_specs = (P(ROW_DEPTH, "col"), P(("row", "col"), None), P())
    return jax.shard_map(body, mesh=finer, in_specs=in_specs, out_specs=out_specs, check_vma=False)
```

profile of v0, /device:TPU:2, one launch (start us, length us, event | category | flops | bytes accessed | tf_op | source)
XLA Modules:
  0.0 152.0 jit_solution(16458376474952683719)
XLA Ops:
  0.6 1.7 %slice.12 = f32[512,1024]{1,0:T(8,128)S(1)} slice(f32[1024,1024]{1,0:T(8,128)} %near_ref.3), slice={[0:512], [0:1024]} | slice | bytes 4194304 | tf_op jit(solution)/shard_map/slice | solution.py:364
  2.4 3.1 %collective-permute-start.4 = (f32[512,1024]{1,0:T(8,128)S(1)}, f32[512,1024]{1,0:T(8,128)}, u32[]{:S(2)}, u32[]{:S(2)}) collective-permute-start(f32[512,1024]{1,0:T(8,128)S(1)} %slice.12), channel_id=1, source_target_pairs={{0,128},{1,129},{2,130},{3,131},{4,132},{5,133},{6,134},{7,135},{8... | collective-permute-start | bytes 6291464 | tf_op jit(solution)/shard_map/ppermute | solution.py:364
  6.1 1.9 %collective-permute-done.4.top_in_ref = f32[512,1024]{1,0:T(8,128)} collective-permute-done((f32[512,1024]{1,0:T(8,128)S(1)}, f32[512,1024]{1,0:T(8,128)}, u32[]{:S(2)}, u32[]{:S(2)}) %collective-permute-start.4) | collective-permute-done | bytes 2097184 | tf_op jit(solution)/shard_map/ppermute | solution.py:364
  8.0 6.1 %shard_map.50 = f32[32,7,8,128]{3,2,1,0:T(8,128)} custom-call(s32[4]{0:T(128)} %pad_add_fusion.place_ref, f32[1024,1024]{1,0:T(8,128)} %near_ref.3, f32[512,1024]{1,0:T(8,128)} %collective-permute-done.4.top_in_ref), custom_call_target="tpu_custom_call" | custom-call | flops 8000000000 | bytes 4000000 | tf_op jit(solution)/shard_map/pallas_call | solution.py:368
  14.1 11.5 %all-to-all-start.1 = ((f32[32,7,8,128]{3,2,1,0:T(8,128)}), f32[32,7,8,128]{3,2,1,0:T(8,128)S(1)}, u32[]{:S(2)}, u32[]{:S(2)}) async-start(f32[32,7,8,128]{3,2,1,0:T(8,128)} %shard_map.50), calls=%async_computation.1 | async-start | bytes 1835008 | tf_op jit(solution)/shard_map/all_to_all | solution.py:342
  25.6 2.6 %shard_map.51 = (f32[11,8,128]{2,1,0:T(8,128)}, f32[11,8,128]{2,1,0:T(8,128)}, f32[11,8,128]{2,1,0:T(8,128)}, f32[11,8,128]{2,1,0:T(8,128)}) custom-call(s32[4]{0:T(128)} %pad_add_fusion.place_ref, f32[1024,512]{1,0:T(8,128)} %a_ref.1), custom_call_target="tpu_custom_call" | custom-call | flops 1000000000 | bytes 4000000 | tf_op jit(solution)/shard_map/pallas_call | solution.py:382
  28.8 2.4 %collective-permute-start.6 = (f32[11,8,128]{2,1,0:T(8,128)}, f32[11,8,128]{2,1,0:T(8,128)S(1)}, u32[]{:S(2)}, u32[]{:S(2)}) collective-permute-start(f32[11,8,128]{2,1,0:T(8,128)} %get-tuple-element.19), channel_id=1, source_target_pairs={{0,64},{32,96},{64,0},{96,32},{1,65},{33,97},{65,1},{97,33},{2,66}... | collective-permute-start | bytes 135176 | tf_op jit(solution)/shard_map/ppermute | solution.py:347
  31.2 1.8 %collective-permute-start.5 = (f32[11,8,128]{2,1,0:T(8,128)}, f32[11,8,128]{2,1,0:T(8,128)S(1)}, u32[]{:S(2)}, u32[]{:S(2)}) collective-permute-start(f32[11,8,128]{2,1,0:T(8,128)} %get-tuple-element.18), channel_id=1, source_target_pairs={{0,32},{32,64},{64,96},{96,0},{1,33},{33,65},{65,97},{97,1},{2,34}... | collective-permute-start | bytes 135176 | tf_op jit(solution)/shard_map/ppermute | solution.py:347
  33.0 1.5 %collective-permute-done.6 = f32[11,8,128]{2,1,0:T(8,128)S(1)} collective-permute-done((f32[11,8,128]{2,1,0:T(8,128)}, f32[11,8,128]{2,1,0:T(8,128)S(1)}, u32[]{:S(2)}, u32[]{:S(2)}) %collective-permute-start.6) | collective-permute-done | bytes 45088 | tf_op jit(solution)/shard_map/ppermute | solution.py:347
  36.3 1.3 collective-permute-start.8
  38.4 13.0 %all-to-all-done.1.got_ref = f32[32,7,8,128]{3,2,1,0:T(8,128)S(1)} async-done(((f32[32,7,8,128]{3,2,1,0:T(8,128)}), f32[32,7,8,128]{3,2,1,0:T(8,128)S(1)}, u32[]{:S(2)}, u32[]{:S(2)}) %all-to-all-start.1) | async-done | bytes 917536 | tf_op jit(solution)/shard_map/all_to_all | solution.py:342
  51.4 1.0 copy-done.1
  52.4 2.3 %shard_map.52 = f32[32,7,8,128]{3,2,1,0:T(8,128)} custom-call(s32[4]{0:T(128)} %pad_add_fusion.place_ref, f32[32,7,8,128]{3,2,1,0:T(8,128)} %copy-done.1, f32[11,8,128]{2,1,0:T(8,128)} %copy-done.2, f32[3,8,128]{2,1,0:T(8,128)} %copy-done.4), custom_call_target="tpu_custom_call" | custom-call | flops 1000000000 | bytes 4000000 | tf_op jit(solution)/shard_map/pallas_call | solution.py:398
  54.7 5.5 %all-to-all-start.2 = ((f32[32,7,8,128]{3,2,1,0:T(8,128)}), f32[32,7,8,128]{3,2,1,0:T(8,128)S(1)}, u32[]{:S(2)}, u32[]{:S(2)}) async-start(f32[32,7,8,128]{3,2,1,0:T(8,128)} %shard_map.52), calls=%async_computation.2 | async-start | bytes 1835008 | tf_op jit(solution)/shard_map/all_to_all | solution.py:342
  60.2 8.6 %shard_map.49 = (f32[8,16,8,128]{3,2,1,0:T(8,128)}, f32[8,16,8,128]{3,2,1,0:T(8,128)}, f32[8,16,8,128]{3,2,1,0:T(8,128)}, f32[8,16,8,128]{3,2,1,0:T(8,128)}) custom-call(s32[4]{0:T(128)} %pad_add_fusion.place_ref, f32[1024,1024]{1,0:T(8,128)} %near_ref.3, f32[1024,1024]{1,0:T(8,128)} %near_ref.3, f32[1024,1024]{1,0:T(8,128)} %collective-permute-done.far_ref), custom_call_target="tpu_custom_call" | custom-call | flops 20000000000 | bytes 4000000 | tf_op jit(solution)/shard_map/pallas_call | solution.py:405
  68.8 3.1 %collective-permute-start.3 = (f32[8,16,8,128]{3,2,1,0:T(8,128)}, f32[8,16,8,128]{3,2,1,0:T(8,128)S(1)}, u32[]{:S(2)}, u32[]{:S(2)}) collective-permute-start(f32[8,16,8,128]{3,2,1,0:T(8,128)} %get-tuple-element.16), channel_id=1, source_target_pairs={{0,3},{1,0},{2,1},{3,2},{4,7},{5,4},{6,5},{7,6},{8,11},{9,8},{10,9... | collective-permute-start | bytes 1572872 | tf_op jit(solution)/shard_map/ppermute | solution.py:347
  73.7 23.7 %collective-permute-done.3 = f32[8,16,8,128]{3,2,1,0:T(8,128)S(1)} collective-permute-done((f32[8,16,8,128]{3,2,1,0:T(8,128)}, f32[8,16,8,128]{3,2,1,0:T(8,128)S(1)}, u32[]{:S(2)}, u32[]{:S(2)}) %collective-permute-start.3) | collective-permute-done | bytes 524320 | tf_op jit(solution)/shard_map/ppermute | solution.py:347
  97.3 4.2 %collective-permute-done.1 = f32[8,16,8,128]{3,2,1,0:T(8,128)S(1)} collective-permute-done((f32[8,16,8,128]{3,2,1,0:T(8,128)}, f32[8,16,8,128]{3,2,1,0:T(8,128)S(1)}, u32[]{:S(2)}, u32[]{:S(2)}) %collective-permute-start.1) | collective-permute-done | bytes 524320 | tf_op jit(solution)/shard_map/ppermute | solution.py:347
  101.5 1.9 %add_add_fusion = f32[8,16,8,128]{3,2,1,0:T(8,128)} fusion(f32[8,16,8,128]{3,2,1,0:T(8,128)S(1)} %collective-permute-done.3, f32[8,16,8,128]{3,2,1,0:T(8,128)S(1)} %collective-permute-done.2, f32[8,16,8,128]{3,2,1,0:T(8,128)} %get-tuple-element.13, f32[8,16,8,128]{3,2,1,0:T(8,128)S(1)} %collective-permute-done.1), kind=kLoop, calls=%fused_computation | loop fusion | flops 393216 | bytes 2621440 | tf_op jit(solution)/shard_map/add | solution.py:420
  103.4 5.6 %all-to-all-start = ((f32[8,16,8,128]{3,2,1,0:T(8,128)}), f32[8,16,8,128]{3,2,1,0:T(8,128)S(1)}, u32[]{:S(2)}, u32[]{:S(2)}) async-start(f32[8,16,8,128]{3,2,1,0:T(8,128)} %add_add_fusion), calls=%async_computation | async-start | bytes 1048576 | tf_op jit(solution)/shard_map/all_to_all | solution.py:342
  109.2 17.4 %all-to-all-done = f32[8,16,8,128]{3,2,1,0:T(8,128)S(1)} async-done(((f32[8,16,8,128]{3,2,1,0:T(8,128)}), f32[8,16,8,128]{3,2,1,0:T(8,128)S(1)}, u32[]{:S(2)}, u32[]{:S(2)}) %all-to-all-start) | async-done | bytes 524320 | tf_op jit(solution)/shard_map/all_to_all | solution.py:342
  126.6 1.5 dynamic-slice_subtract_fusion
  128.8 22.0 %shard_map.53 = (f32[256,512]{1,0:T(8,128)}, f32[8,128]{1,0:T(8,128)}) custom-call(s32[4]{0:T(128)} %pad_add_fusion.place_ref, f32[32,7,8,128]{3,2,1,0:T(8,128)} %copy-done, f32[32,3,8,128]{3,2,1,0:T(8,128)} %copy-done.3), custom_call_target="tpu_custom_call" | custom-call | flops 30000001024 | bytes 4000000 | tf_op jit(solution)/shard_map/pallas_call | solution.py:426
  150.8 1.2 slice.15
  (26 shorter events, 6.5 us)
Async XLA Ops:
  2.4 5.6 %collective-permute-start.4 = (f32[512,1024]{1,0:T(8,128)S(1)}, f32[512,1024]{1,0:T(8,128)}, u32[]{:S(2)}, u32[]{:S(2)}) collective-permute-start(f32[512,1024]{1,0:T(8,128)S(1)} %slice.12), channel_id=1, source_target_pairs={{0,128},{1,129},{2,130},{3,131},{4,132},{5,133},{6,134},{7,135},{8... | collective-permute-start | bytes 6291464 | tf_op jit(solution)/shard_map/ppermute | solution.py:364
  5.5 54.8 %collective-permute-start = (f32[1024,1024]{1,0:T(8,128)}, f32[1024,1024]{1,0:T(8,128)}, u32[]{:S(2)}, u32[]{:S(2)}) collective-permute-start(f32[1024,1024]{1,0:T(8,128)} %near_ref.3), channel_id=1, source_target_pairs={{0,128},{128,0},{1,129},{129,1},{2,130},{130,2},{3,131},{131,3},{4... | collective-permute-start | bytes 12582920 | tf_op jit(solution)/shard_map/ppermute | solution.py:365
  14.1 37.3 %all-to-all-start.1 = ((f32[32,7,8,128]{3,2,1,0:T(8,128)}), f32[32,7,8,128]{3,2,1,0:T(8,128)S(1)}, u32[]{:S(2)}, u32[]{:S(2)}) async-start(f32[32,7,8,128]{3,2,1,0:T(8,128)} %shard_map.50), calls=%async_computation.1 | async-start | bytes 1835008 | tf_op jit(solution)/shard_map/all_to_all | solution.py:342
  28.2 4.8 %collective-permute-start.7 = (f32[11,8,128]{2,1,0:T(8,128)}, f32[11,8,128]{2,1,0:T(8,128)S(1)}, u32[]{:S(2)}, u32[]{:S(2)}) collective-permute-start(f32[11,8,128]{2,1,0:T(8,128)} %get-tuple-element.20), channel_id=1, source_target_pairs={{0,96},{32,0},{64,32},{96,64},{1,97},{33,1},{65,33},{97,65},{2,98}... | collective-permute-start | bytes 135176 | tf_op jit(solution)/shard_map/ppermute | solution.py:347
  28.8 5.8 %collective-permute-start.6 = (f32[11,8,128]{2,1,0:T(8,128)}, f32[11,8,128]{2,1,0:T(8,128)S(1)}, u32[]{:S(2)}, u32[]{:S(2)}) collective-permute-start(f32[11,8,128]{2,1,0:T(8,128)} %get-tuple-element.19), channel_id=1, source_target_pairs={{0,64},{32,96},{64,0},{96,32},{1,65},{33,97},{65,1},{97,33},{2,66}... | collective-permute-start | bytes 135176 | tf_op jit(solution)/shard_map/ppermute | solution.py:347
  31.2 4.3 %collective-permute-start.5 = (f32[11,8,128]{2,1,0:T(8,128)}, f32[11,8,128]{2,1,0:T(8,128)S(1)}, u32[]{:S(2)}, u32[]{:S(2)}) collective-permute-start(f32[11,8,128]{2,1,0:T(8,128)} %get-tuple-element.18), channel_id=1, source_target_pairs={{0,32},{32,64},{64,96},{96,0},{1,33},{33,65},{65,97},{97,1},{2,34}... | collective-permute-start | bytes 135176 | tf_op jit(solution)/shard_map/ppermute | solution.py:347
  36.3 15.1 %copy-start.2 = (f32[11,8,128]{2,1,0:T(8,128)}, f32[11,8,128]{2,1,0:T(8,128)S(1)}, u32[]{:S(2)}) copy-start(f32[11,8,128]{2,1,0:T(8,128)S(1)} %add_add_fusion.1.a_ref) | copy-start | bytes 135172
  36.3 2.1 %collective-permute-start.8 = (f32[3,8,128]{2,1,0:T(8,128)S(1)}, f32[3,8,128]{2,1,0:T(8,128)S(1)}, u32[]{:S(2)}, u32[]{:S(2)}) collective-permute-start(f32[3,8,128]{2,1,0:T(8,128)S(1)} %slice.16), channel_id=1, source_target_pairs={{0,128},{1,129},{2,130},{3,131},{4,132},{5,133},{6,134},{7,135},{8... | collective-permute-start | bytes 36872 | tf_op jit(solution)/shard_map/ppermute | solution.py:396
  38.4 13.0 %copy-start.4 = (f32[3,8,128]{2,1,0:T(8,128)}, f32[3,8,128]{2,1,0:T(8,128)S(1)}, u32[]{:S(2)}) copy-start(f32[3,8,128]{2,1,0:T(8,128)S(1)} %collective-permute-done.8.other_ref) | copy-start | bytes 36868
  51.4 1.0 copy-start.1
  54.7 48.8 %all-to-all-start.2 = ((f32[32,7,8,128]{3,2,1,0:T(8,128)}), f32[32,7,8,128]{3,2,1,0:T(8,128)S(1)}, u32[]{:S(2)}, u32[]{:S(2)}) async-start(f32[32,7,8,128]{3,2,1,0:T(8,128)} %shard_map.52), calls=%async_computation.2 | async-start | bytes 1835008 | tf_op jit(solution)/shard_map/all_to_all | solution.py:342
  68.8 28.5 %collective-permute-start.3 = (f32[8,16,8,128]{3,2,1,0:T(8,128)}, f32[8,16,8,128]{3,2,1,0:T(8,128)S(1)}, u32[]{:S(2)}, u32[]{:S(2)}) collective-permute-start(f32[8,16,8,128]{3,2,1,0:T(8,128)} %get-tuple-element.16), channel_id=1, source_target_pairs={{0,3},{1,0},{2,1},{3,2},{4,7},{5,4},{6,5},{7,6},{8,11},{9,8},{10,9... | collective-permute-start | bytes 1572872 | tf_op jit(solution)/shard_map/ppermute | solution.py:347
  71.9 25.4 %collective-permute-start.2 = (f32[8,16,8,128]{3,2,1,0:T(8,128)}, f32[8,16,8,128]{3,2,1,0:T(8,128)S(1)}, u32[]{:S(2)}, u32[]{:S(2)}) collective-permute-start(f32[8,16,8,128]{3,2,1,0:T(8,128)} %get-tuple-element.15), channel_id=1, source_target_pairs={{0,2},{1,3},{2,0},{3,1},{4,6},{5,7},{6,4},{7,5},{8,10},{9,11},{10,... | collective-permute-start | bytes 1572872 | tf_op jit(solution)/shard_map/ppermute | solution.py:347
  72.8 28.7 %collective-permute-start.1 = (f32[8,16,8,128]{3,2,1,0:T(8,128)}, f32[8,16,8,128]{3,2,1,0:T(8,128)S(1)}, u32[]{:S(2)}, u32[]{:S(2)}) collective-permute-start(f32[8,16,8,128]{3,2,1,0:T(8,128)} %get-tuple-element.14), channel_id=1, source_target_pairs={{0,1},{1,2},{2,3},{3,0},{4,5},{5,6},{6,7},{7,4},{8,9},{9,10},{10,1... | collective-permute-start | bytes 1572872 | tf_op jit(solution)/shard_map/ppermute | solution.py:347
  103.4 24.6 %copy-start = (f32[32,7,8,128]{3,2,1,0:T(8,128)}, f32[32,7,8,128]{3,2,1,0:T(8,128)S(1)}, u32[]{:S(2)}) copy-start(f32[32,7,8,128]{3,2,1,0:T(8,128)S(1)} %all-to-all-done.2.mine_ref) | copy-start | bytes 2752516
  103.4 23.1 %all-to-all-start = ((f32[8,16,8,128]{3,2,1,0:T(8,128)}), f32[8,16,8,128]{3,2,1,0:T(8,128)S(1)}, u32[]{:S(2)}, u32[]{:S(2)}) async-start(f32[8,16,8,128]{3,2,1,0:T(8,128)} %add_add_fusion), calls=%async_computation | async-start | bytes 1048576 | tf_op jit(solution)/shard_map/all_to_all | solution.py:342
  109.1 19.0 %collective-permute-start.9 = (f32[32,3,8,128]{3,2,1,0:T(8,128)S(1)}, f32[32,3,8,128]{3,2,1,0:T(8,128)S(1)}, u32[]{:S(2)}, u32[]{:S(2)}) collective-permute-start(f32[32,3,8,128]{3,2,1,0:T(8,128)S(1)} %slice.17), channel_id=1, source_target_pairs={{0,128},{128,0},{1,129},{129,1},{2,130},{130,2},{3,131},{131,3},{4... | collective-permute-start | bytes 1179656 | tf_op jit(solution)/shard_map/ppermute | solution.py:402
  128.1 0.8 copy-start.3
where the time goes:
time: 154 us; the launch traced here: 152 us
  waiting for transfers between devices  63.4 us (41%)
  Pallas kernels  41.5 us (27%)
  starting transfers between devices  36.8 us (24%)
  other arithmetic  4.92 us (3%)
  local copies, waits for them, and re-layouts  4.69 us (3%)
    all_to_all x3, waiting for transfers between devices, exchange(): return lax.all_to_all(pieces, axis, split_axis=0, concat_axis=0, tiled=True)  30.4 us
    ppermute x6, waiting for transfers between devices, shifted(): lax.ppermute(value, axis, [(i, (i + by) % size) for i in range(size)])  30.3 us
    all_to_all x3, starting transfers between devices, exchange(): return lax.all_to_all(pieces, axis, split_axis=0, concat_axis=0, tiled=True)  22.6 us
    pallas_call x1, Pallas kernels, body(): call(solve_kernel, 30000000000, [shaped(c_rows, PB), shaped(*TILE)], [SME...  22 us
    ppermute x6, starting transfers between devices, shifted(): lax.ppermute(value, axis, [(i, (i + by) % size) for i in range(size)])  9.64 us
    pallas_call x1, Pallas kernels, body(): call(block_kernel, 20000000000, [piece] * Y_SIZE, [SMEM, pl.BlockSpec((PB...  8.6 us
    pallas_call x1, Pallas kernels, body(): call(top_kernel, 8000000000, [piece], [SMEM, ANY, ANY], [pltpu.VMEM((c_ro...  6.07 us
    ppermute x1, starting transfers between devices, body(): top = lax.ppermute(panels[:PB], 'row', [(0, 1)])  3.1 us
  transfers between devices with their start and end apart: 13, of which 8 were waited for; matrix products, arithmetic and copies ran while one was open for 3% of the time, Pallas kernels for 13%

commit v1 on v0

--- a/solution.py
+++ b/solution.py
@@ -267,7 +267,7 @@
     return slice(LANES * i, LANES * (i + 1))
 
 
-def solve_kernel(place_ref, mine_ref, other_ref, x_ref, norm_ref, w, inv_ref):
+def solve_kernel(place_ref, mine_ref, other_ref, x_ref, norm_ref, w):
     r = place_ref[0]
     for half in range(2):
         for ref, take in ((mine_ref, r == half), (other_ref, r != half)):
@@ -286,34 +286,40 @@
     total = mine_ref[SUM_PIECE, SUM_SLOT] + other_ref[SUM_PIECE, SUM_SLOT]
     norm_ref[...] = jnp.sqrt(total / 2048.0)
 
-    def step(b, carry):
-        start = (b * (b + 3)) // 2 * LANES
-
-        def load(h):
-            return w[pl.ds(pl.multiple_of(start + SUBLANES * h, SUBLANES), SUBLANES)]
-
-        def store(h, value):
-            inv_ref[SUBLANES * h : SUBLANES * (h + 1)] = value
-
-        inverse_factor(load, store)
-        for s in range(BLOCKS):
-
-            @pl.when(b == s)
-            def _(s=s):
-                inv = inv_ref[...]
-                for i in range(s + 1, BLOCKS):
-                    w[at(i, s)] = times_transposed(w[at(i, s)], inv)
-                for j in range(s + 1, BLOCKS):
-                    for i in range(j, BLOCKS):
-                        w[at(i, j)] = w[at(i, j)] - times_transposed(w[at(i, s)], w[at(j, s)])
-                x = times_transposed(x_ref[:, block(s)], inv)
-                x_ref[:, block(s)] = x
-                for j in range(s + 1, BLOCKS):
-                    x_ref[:, block(j)] = x_ref[:, block(j)] - times_transposed(x, w[at(j, s)])
-
-        return carry
-
-    lax.fori_loop(0, BLOCKS, step, 0)
+    low = {(i, j): w[at(i, j)] for i in range(BLOCKS) for j in range(i + 1)}
+    rows = [x_ref[:, block(l)] for l in range(WIDE)]
+    for s in range(BLOCKS):
+        parts = [None] * GROUPS
+
+        def load(h, square=low[s, s]):
+            return square[SUBLANES * h : SUBLANES * (h + 1)]
+
+        inverse_factor(load, parts.__setitem__)
+        inv = jnp.concatenate(parts)
+        for i in range(s + 1, BLOCKS):
+            low[i, s] = times_transposed(low[i, s], inv)
+        for j in range(s + 1, BLOCKS):
+            for i in range(j, BLOCKS):
+                low[i, j] = low[i, j] - times_transposed(low[i, s], low[j, s])
+        x = times_transposed(rows[s], inv)
+        x_ref[:, block(s)] = x
+        for j in range(s + 1, BLOCKS):
+            rows[j] = rows[j] - times_transposed(x, low[j, s])
+
+
+def trailing_kernel(place_ref, got_ref, a_ref, out_ref, a_buf, sem):
+    share = out_ref.shape[0]
+    row = pl.multiple_of((place_ref[2] * Y_SIZE + place_ref[3]) * share, share)
+    copy = pltpu.make_async_copy(a_ref.at[pl.ds(row, share)], a_buf, sem)
+    copy.start()
+    copy.wait()
+    for g in range(share // SUBLANES):
+        for l in range(WIDE):
+            total = got_ref[0, g * WIDE + l]
+            for n in range(1, got_ref.shape[0]):
+                total = total + got_ref[n, g * WIDE + l]
+            here = (slice(SUBLANES * g, SUBLANES * (g + 1)), slice(LANES * l, LANES * (l + 1)))
+            out_ref[here] = a_buf[here] - total
 
 
 SMEM = pl.BlockSpec(memory_space=pltpu.SMEM)
@@ -357,7 +363,7 @@
     c_rows = tile_rows // 4
     share = tile_rows // depth
     k_size = panels.shape[1]
-    r, c, d = lax.axis_index("row"), lax.axis_index("col"), lax.axis_index(DEPTH)
+    r, c = lax.axis_index("row"), lax.axis_index("col")
     place = jnp.stack([r, c, lax.axis_index(Z), lax.axis_index(Y)]).astype(jnp.int32)
     swap = [(0, 1), (1, 0)]
 
@@ -419,16 +425,20 @@
     parts = delivered(parts, Y)
     part = sum(parts)
     got = exchange(part, Z)
-    tiles = got.sum(axis=0)
-    tiles = tiles.reshape(4, WIDE, *TILE).transpose(0, 2, 1, 3).reshape(share, tile_cols)
-    trailing = lax.dynamic_slice_in_dim(a_tile, d * share, share, 0) - tiles
+    (trailing,) = call(
+        trailing_kernel,
+        1_000_000_000,
+        [shaped(share, tile_cols)],
+        [SMEM, VMEM, ANY],
+        [pltpu.VMEM((share, tile_cols), F32), pltpu.SemaphoreType.DMA],
+    )(place, got, a_tile)
 
     new_panel, norm = call(
         solve_kernel,
         30_000_000_000,
         [shaped(c_rows, PB), shaped(*TILE)],
         [SMEM, VMEM, VMEM],
-        [pltpu.VMEM((PAIRS * LANES, LANES), F32), pltpu.VMEM((LANES, LANES), F32)],
+        [pltpu.VMEM((PAIRS * LANES, LANES), F32)],
     )(place, mine, other)
     return (trailing, new_panel, norm[0, :1])
 

time: 154 us -> 154 us (level)
  other arithmetic: 4.92 us -> 3.38 us
    pallas_call x0 -> x1, Pallas kernels: none -> 2.56 us  [body(): call(trailing_kernel, 1000000000, [shaped(share, tile_cols)], [SMEM, VMEM...]
  transfers between devices with their start and end apart: 13 -> 13, of which waited for: 8 -> 8; matrix products, arithmetic and copies ran while one was open for 3% -> 2% of each run, Pallas kernels for 13% -> 15%
where the time goes in v1:
time: 154 us; the launch traced here: 153 us
  waiting for transfers between devices  63.4 us (41%)
  Pallas kernels  42.9 us (28%)
  starting transfers between devices  36.7 us (24%)
  local copies, waits for them, and re-layouts  5.46 us (4%)
  other arithmetic  3.38 us (2%)
    all_to_all x3, waiting for transfers between devices, exchange(): return lax.all_to_all(pieces, axis, split_axis=0, concat_axis=0, tiled=True)  30.4 us
    ppermute x6, waiting for transfers between devices, shifted(): lax.ppermute(value, axis, [(i, (i + by) % size) for i in range(size)])  30.3 us
    all_to_all x3, starting transfers between devices, exchange(): return lax.all_to_all(pieces, axis, split_axis=0, concat_axis=0, tiled=True)  22.6 us
    pallas_call x1, Pallas kernels, body(): call(solve_kernel, 30000000000, [shaped(c_rows, PB), shaped(*TILE)], [SME...  20.7 us
    ppermute x6, starting transfers between devices, shifted(): lax.ppermute(value, axis, [(i, (i + by) % size) for i in range(size)])  9.64 us
    pallas_call x1, Pallas kernels, body(): call(block_kernel, 20000000000, [piece] * Y_SIZE, [SMEM, pl.BlockSpec((PB...  8.62 us
    pallas_call x1, Pallas kernels, body(): call(top_kernel, 8000000000, [piece], [SMEM, ANY, ANY], [pltpu.VMEM((c_ro...  6.06 us
    ppermute x1, starting transfers between devices, body(): top = lax.ppermute(panels[:PB], 'row', [(0, 1)])  3.08 us
  transfers between devices with their start and end apart: 13, of which 8 were waited for; matrix products, arithmetic and copies ran while one was open for 2% of the time, Pallas kernels for 15%

profile of v1, /device:TPU:2, one launch (start us, length us, event | category | flops | bytes accessed | tf_op | source)
XLA Modules:
  0.0 152.6 jit_solution(8899324157074600329)
XLA Ops:
  0.6 1.7 %slice.12 = f32[512,1024]{1,0:T(8,128)S(1)} slice(f32[1024,1024]{1,0:T(8,128)} %near_ref.3), slice={[0:512], [0:1024]} | slice | bytes 4194304 | tf_op jit(solution)/shard_map/slice | solution.py:370
  2.4 3.1 %collective-permute-start.4 = (f32[512,1024]{1,0:T(8,128)S(1)}, f32[512,1024]{1,0:T(8,128)}, u32[]{:S(2)}, u32[]{:S(2)}) collective-permute-start(f32[512,1024]{1,0:T(8,128)S(1)} %slice.12), channel_id=1, source_target_pairs={{0,128},{1,129},{2,130},{3,131},{4,132},{5,133},{6,134},{7,135},{8... | collective-permute-start | bytes 6291464 | tf_op jit(solution)/shard_map/ppermute | solution.py:370
  6.1 1.9 %collective-permute-done.4.top_in_ref = f32[512,1024]{1,0:T(8,128)} collective-permute-done((f32[512,1024]{1,0:T(8,128)S(1)}, f32[512,1024]{1,0:T(8,128)}, u32[]{:S(2)}, u32[]{:S(2)}) %collective-permute-start.4) | collective-permute-done | bytes 2097184 | tf_op jit(solution)/shard_map/ppermute | solution.py:370
  8.0 6.1 %shard_map.51 = f32[32,7,8,128]{3,2,1,0:T(8,128)} custom-call(s32[4]{0:T(128)} %pad_add_fusion.place_ref, f32[1024,1024]{1,0:T(8,128)} %near_ref.3, f32[512,1024]{1,0:T(8,128)} %collective-permute-done.4.top_in_ref), custom_call_target="tpu_custom_call" | custom-call | flops 8000000000 | bytes 4000000 | tf_op jit(solution)/shard_map/pallas_call | solution.py:374
  14.1 11.5 %all-to-all-start.1 = ((f32[32,7,8,128]{3,2,1,0:T(8,128)}), f32[32,7,8,128]{3,2,1,0:T(8,128)S(1)}, u32[]{:S(2)}, u32[]{:S(2)}) async-start(f32[32,7,8,128]{3,2,1,0:T(8,128)} %shard_map.51), calls=%async_computation.1 | async-start | bytes 1835008 | tf_op jit(solution)/shard_map/all_to_all | solution.py:348
  25.6 2.6 %shard_map.52 = (f32[11,8,128]{2,1,0:T(8,128)}, f32[11,8,128]{2,1,0:T(8,128)}, f32[11,8,128]{2,1,0:T(8,128)}, f32[11,8,128]{2,1,0:T(8,128)}) custom-call(s32[4]{0:T(128)} %pad_add_fusion.place_ref, f32[1024,512]{1,0:T(8,128)} %a_ref.3), custom_call_target="tpu_custom_call" | custom-call | flops 1000000000 | bytes 4000000 | tf_op jit(solution)/shard_map/pallas_call | solution.py:388
  28.8 2.4 %collective-permute-start.6 = (f32[11,8,128]{2,1,0:T(8,128)}, f32[11,8,128]{2,1,0:T(8,128)S(1)}, u32[]{:S(2)}, u32[]{:S(2)}) collective-permute-start(f32[11,8,128]{2,1,0:T(8,128)} %get-tuple-element.19), channel_id=1, source_target_pairs={{0,64},{32,96},{64,0},{96,32},{1,65},{33,97},{65,1},{97,33},{2,66}... | collective-permute-start | bytes 135176 | tf_op jit(solution)/shard_map/ppermute | solution.py:353
  31.2 1.8 %collective-permute-start.5 = (f32[11,8,128]{2,1,0:T(8,128)}, f32[11,8,128]{2,1,0:T(8,128)S(1)}, u32[]{:S(2)}, u32[]{:S(2)}) collective-permute-start(f32[11,8,128]{2,1,0:T(8,128)} %get-tuple-element.18), channel_id=1, source_target_pairs={{0,32},{32,64},{64,96},{96,0},{1,33},{33,65},{65,97},{97,1},{2,34}... | collective-permute-start | bytes 135176 | tf_op jit(solution)/shard_map/ppermute | solution.py:353
  33.0 1.5 %collective-permute-done.6 = f32[11,8,128]{2,1,0:T(8,128)S(1)} collective-permute-done((f32[11,8,128]{2,1,0:T(8,128)}, f32[11,8,128]{2,1,0:T(8,128)S(1)}, u32[]{:S(2)}, u32[]{:S(2)}) %collective-permute-start.6) | collective-permute-done | bytes 45088 | tf_op jit(solution)/shard_map/ppermute | solution.py:353
  36.3 1.3 collective-permute-start.8
  38.4 13.0 %all-to-all-done.1.got_ref = f32[32,7,8,128]{3,2,1,0:T(8,128)S(1)} async-done(((f32[32,7,8,128]{3,2,1,0:T(8,128)}), f32[32,7,8,128]{3,2,1,0:T(8,128)S(1)}, u32[]{:S(2)}, u32[]{:S(2)}) %all-to-all-start.1) | async-done | bytes 917536 | tf_op jit(solution)/shard_map/all_to_all | solution.py:348
  51.4 1.0 copy-done.1
  52.4 2.3 %shard_map.53 = f32[32,7,8,128]{3,2,1,0:T(8,128)} custom-call(s32[4]{0:T(128)} %pad_add_fusion.place_ref, f32[32,7,8,128]{3,2,1,0:T(8,128)} %copy-done.1, f32[11,8,128]{2,1,0:T(8,128)} %copy-done.3, f32[3,8,128]{2,1,0:T(8,128)} %copy-done.5), custom_call_target="tpu_custom_call" | custom-call | flops 1000000000 | bytes 4000000 | tf_op jit(solution)/shard_map/pallas_call | solution.py:404
  54.7 5.5 %all-to-all-start.2 = ((f32[32,7,8,128]{3,2,1,0:T(8,128)}), f32[32,7,8,128]{3,2,1,0:T(8,128)S(1)}, u32[]{:S(2)}, u32[]{:S(2)}) async-start(f32[32,7,8,128]{3,2,1,0:T(8,128)} %shard_map.53), calls=%async_computation.2 | async-start | bytes 1835008 | tf_op jit(solution)/shard_map/all_to_all | solution.py:348
  60.2 8.6 %shard_map.49 = (f32[8,16,8,128]{3,2,1,0:T(8,128)}, f32[8,16,8,128]{3,2,1,0:T(8,128)}, f32[8,16,8,128]{3,2,1,0:T(8,128)}, f32[8,16,8,128]{3,2,1,0:T(8,128)}) custom-call(s32[4]{0:T(128)} %pad_add_fusion.place_ref, f32[1024,1024]{1,0:T(8,128)} %near_ref.3, f32[1024,1024]{1,0:T(8,128)} %near_ref.3, f32[1024,1024]{1,0:T(8,128)} %collective-permute-done.far_ref), custom_call_target="tpu_custom_call" | custom-call | flops 20000000000 | bytes 4000000 | tf_op jit(solution)/shard_map/pallas_call | solution.py:411
  68.9 3.1 %collective-permute-start.3 = (f32[8,16,8,128]{3,2,1,0:T(8,128)}, f32[8,16,8,128]{3,2,1,0:T(8,128)S(1)}, u32[]{:S(2)}, u32[]{:S(2)}) collective-permute-start(f32[8,16,8,128]{3,2,1,0:T(8,128)} %get-tuple-element.16), channel_id=1, source_target_pairs={{0,3},{1,0},{2,1},{3,2},{4,7},{5,4},{6,5},{7,6},{8,11},{9,8},{10,9... | collective-permute-start | bytes 1572872 | tf_op jit(solution)/shard_map/ppermute | solution.py:353
  73.7 23.7 %collective-permute-done.3 = f32[8,16,8,128]{3,2,1,0:T(8,128)S(1)} collective-permute-done((f32[8,16,8,128]{3,2,1,0:T(8,128)}, f32[8,16,8,128]{3,2,1,0:T(8,128)S(1)}, u32[]{:S(2)}, u32[]{:S(2)}) %collective-permute-start.3) | collective-permute-done | bytes 524320 | tf_op jit(solution)/shard_map/ppermute | solution.py:353
  97.4 4.1 %collective-permute-done.1 = f32[8,16,8,128]{3,2,1,0:T(8,128)S(1)} collective-permute-done((f32[8,16,8,128]{3,2,1,0:T(8,128)}, f32[8,16,8,128]{3,2,1,0:T(8,128)S(1)}, u32[]{:S(2)}, u32[]{:S(2)}) %collective-permute-start.1) | collective-permute-done | bytes 524320 | tf_op jit(solution)/shard_map/ppermute | solution.py:353
  101.5 1.9 %add_add_fusion = f32[8,16,8,128]{3,2,1,0:T(8,128)} fusion(f32[8,16,8,128]{3,2,1,0:T(8,128)S(1)} %collective-permute-done.3, f32[8,16,8,128]{3,2,1,0:T(8,128)S(1)} %collective-permute-done.2, f32[8,16,8,128]{3,2,1,0:T(8,128)} %get-tuple-element.13, f32[8,16,8,128]{3,2,1,0:T(8,128)S(1)} %collective-permute-done.1), kind=kLoop, calls=%fused_computation | loop fusion | flops 393216 | bytes 2621440 | tf_op jit(solution)/shard_map/add | solution.py:426
  103.4 5.6 %all-to-all-start = ((f32[8,16,8,128]{3,2,1,0:T(8,128)}), f32[8,16,8,128]{3,2,1,0:T(8,128)S(1)}, u32[]{:S(2)}, u32[]{:S(2)}) async-start(f32[8,16,8,128]{3,2,1,0:T(8,128)} %add_add_fusion), calls=%async_computation | async-start | bytes 1048576 | tf_op jit(solution)/shard_map/all_to_all | solution.py:348
  109.2 17.4 %all-to-all-done.got_ref = f32[8,16,8,128]{3,2,1,0:T(8,128)S(1)} async-done(((f32[8,16,8,128]{3,2,1,0:T(8,128)}), f32[8,16,8,128]{3,2,1,0:T(8,128)S(1)}, u32[]{:S(2)}, u32[]{:S(2)}) %all-to-all-start) | async-done | bytes 524320 | tf_op jit(solution)/shard_map/all_to_all | solution.py:348
  127.4 2.6 %shard_map.50 = f32[32,512]{1,0:T(8,128)} custom-call(s32[4]{0:T(128)} %pad_add_fusion.place_ref, f32[8,16,8,128]{3,2,1,0:T(8,128)} %copy-done.2, f32[1024,512]{1,0:T(8,128)} %a_ref.3), custom_call_target="tpu_custom_call" | custom-call | flops 1000000000 | bytes 4000000 | tf_op jit(solution)/shard_map/pallas_call | solution.py:428
  130.7 20.7 %shard_map.54 = (f32[256,512]{1,0:T(8,128)}, f32[8,128]{1,0:T(8,128)}) custom-call(s32[4]{0:T(128)} %pad_add_fusion.place_ref, f32[32,7,8,128]{3,2,1,0:T(8,128)} %copy-done, f32[32,3,8,128]{3,2,1,0:T(8,128)} %copy-done.4), custom_call_target="tpu_custom_call" | custom-call | flops 30000001024 | bytes 4000000 | tf_op jit(solution)/shard_map/pallas_call | solution.py:436
  151.4 1.2 slice.15
  (27 shorter events, 7.2 us)
Async XLA Ops:
  2.4 5.6 %collective-permute-start.4 = (f32[512,1024]{1,0:T(8,128)S(1)}, f32[512,1024]{1,0:T(8,128)}, u32[]{:S(2)}, u32[]{:S(2)}) collective-permute-start(f32[512,1024]{1,0:T(8,128)S(1)} %slice.12), channel_id=1, source_target_pairs={{0,128},{1,129},{2,130},{3,131},{4,132},{5,133},{6,134},{7,135},{8... | collective-permute-start | bytes 6291464 | tf_op jit(solution)/shard_map/ppermute | solution.py:370
  5.4 54.8 %collective-permute-start = (f32[1024,1024]{1,0:T(8,128)}, f32[1024,1024]{1,0:T(8,128)}, u32[]{:S(2)}, u32[]{:S(2)}) collective-permute-start(f32[1024,1024]{1,0:T(8,128)} %near_ref.3), channel_id=1, source_target_pairs={{0,128},{128,0},{1,129},{129,1},{2,130},{130,2},{3,131},{131,3},{4... | collective-permute-start | bytes 12582920 | tf_op jit(solution)/shard_map/ppermute | solution.py:371
  14.1 37.3 %all-to-all-start.1 = ((f32[32,7,8,128]{3,2,1,0:T(8,128)}), f32[32,7,8,128]{3,2,1,0:T(8,128)S(1)}, u32[]{:S(2)}, u32[]{:S(2)}) async-start(f32[32,7,8,128]{3,2,1,0:T(8,128)} %shard_map.51), calls=%async_computation.1 | async-start | bytes 1835008 | tf_op jit(solution)/shard_map/all_to_all | solution.py:348
  28.2 4.8 %collective-permute-start.7 = (f32[11,8,128]{2,1,0:T(8,128)}, f32[11,8,128]{2,1,0:T(8,128)S(1)}, u32[]{:S(2)}, u32[]{:S(2)}) collective-permute-start(f32[11,8,128]{2,1,0:T(8,128)} %get-tuple-element.20), channel_id=1, source_target_pairs={{0,96},{32,0},{64,32},{96,64},{1,97},{33,1},{65,33},{97,65},{2,98}... | collective-permute-start | bytes 135176 | tf_op jit(solution)/shard_map/ppermute | solution.py:353
  28.8 5.8 %collective-permute-start.6 = (f32[11,8,128]{2,1,0:T(8,128)}, f32[11,8,128]{2,1,0:T(8,128)S(1)}, u32[]{:S(2)}, u32[]{:S(2)}) collective-permute-start(f32[11,8,128]{2,1,0:T(8,128)} %get-tuple-element.19), channel_id=1, source_target_pairs={{0,64},{32,96},{64,0},{96,32},{1,65},{33,97},{65,1},{97,33},{2,66}... | collective-permute-start | bytes 135176 | tf_op jit(solution)/shard_map/ppermute | solution.py:353
  31.2 4.3 %collective-permute-start.5 = (f32[11,8,128]{2,1,0:T(8,128)}, f32[11,8,128]{2,1,0:T(8,128)S(1)}, u32[]{:S(2)}, u32[]{:S(2)}) collective-permute-start(f32[11,8,128]{2,1,0:T(8,128)} %get-tuple-element.18), channel_id=1, source_target_pairs={{0,32},{32,64},{64,96},{96,0},{1,33},{33,65},{65,97},{97,1},{2,34}... | collective-permute-start | bytes 135176 | tf_op jit(solution)/shard_map/ppermute | solution.py:353
  36.3 15.1 %copy-start.3 = (f32[11,8,128]{2,1,0:T(8,128)}, f32[11,8,128]{2,1,0:T(8,128)S(1)}, u32[]{:S(2)}) copy-start(f32[11,8,128]{2,1,0:T(8,128)S(1)} %add_add_fusion.1.a_ref) | copy-start | bytes 135172
  36.3 2.1 %collective-permute-start.8 = (f32[3,8,128]{2,1,0:T(8,128)S(1)}, f32[3,8,128]{2,1,0:T(8,128)S(1)}, u32[]{:S(2)}, u32[]{:S(2)}) collective-permute-start(f32[3,8,128]{2,1,0:T(8,128)S(1)} %slice.16), channel_id=1, source_target_pairs={{0,128},{1,129},{2,130},{3,131},{4,132},{5,133},{6,134},{7,135},{8... | collective-permute-start | bytes 36872 | tf_op jit(solution)/shard_map/ppermute | solution.py:402
  38.4 13.0 %copy-start.5 = (f32[3,8,128]{2,1,0:T(8,128)}, f32[3,8,128]{2,1,0:T(8,128)S(1)}, u32[]{:S(2)}) copy-start(f32[3,8,128]{2,1,0:T(8,128)S(1)} %collective-permute-done.8.other_ref) | copy-start | bytes 36868
  51.4 1.0 copy-start.1
  54.7 48.8 %all-to-all-start.2 = ((f32[32,7,8,128]{3,2,1,0:T(8,128)}), f32[32,7,8,128]{3,2,1,0:T(8,128)S(1)}, u32[]{:S(2)}, u32[]{:S(2)}) async-start(f32[32,7,8,128]{3,2,1,0:T(8,128)} %shard_map.53), calls=%async_computation.2 | async-start | bytes 1835008 | tf_op jit(solution)/shard_map/all_to_all | solution.py:348
  68.9 28.5 %collective-permute-start.3 = (f32[8,16,8,128]{3,2,1,0:T(8,128)}, f32[8,16,8,128]{3,2,1,0:T(8,128)S(1)}, u32[]{:S(2)}, u32[]{:S(2)}) collective-permute-start(f32[8,16,8,128]{3,2,1,0:T(8,128)} %get-tuple-element.16), channel_id=1, source_target_pairs={{0,3},{1,0},{2,1},{3,2},{4,7},{5,4},{6,5},{7,6},{8,11},{9,8},{10,9... | collective-permute-start | bytes 1572872 | tf_op jit(solution)/shard_map/ppermute | solution.py:353
  72.0 25.4 %collective-permute-start.2 = (f32[8,16,8,128]{3,2,1,0:T(8,128)}, f32[8,16,8,128]{3,2,1,0:T(8,128)S(1)}, u32[]{:S(2)}, u32[]{:S(2)}) collective-permute-start(f32[8,16,8,128]{3,2,1,0:T(8,128)} %get-tuple-element.15), channel_id=1, source_target_pairs={{0,2},{1,3},{2,0},{3,1},{4,6},{5,7},{6,4},{7,5},{8,10},{9,11},{10,... | collective-permute-start | bytes 1572872 | tf_op jit(solution)/shard_map/ppermute | solution.py:353
  72.8 28.7 %collective-permute-start.1 = (f32[8,16,8,128]{3,2,1,0:T(8,128)}, f32[8,16,8,128]{3,2,1,0:T(8,128)S(1)}, u32[]{:S(2)}, u32[]{:S(2)}) collective-permute-start(f32[8,16,8,128]{3,2,1,0:T(8,128)} %get-tuple-element.14), channel_id=1, source_target_pairs={{0,1},{1,2},{2,3},{3,0},{4,5},{5,6},{6,7},{7,4},{8,9},{9,10},{10,1... | collective-permute-start | bytes 1572872 | tf_op jit(solution)/shard_map/ppermute | solution.py:353
  103.4 26.5 %copy-start = (f32[32,7,8,128]{3,2,1,0:T(8,128)}, f32[32,7,8,128]{3,2,1,0:T(8,128)S(1)}, u32[]{:S(2)}) copy-start(f32[32,7,8,128]{3,2,1,0:T(8,128)S(1)} %all-to-all-done.2.mine_ref) | copy-start | bytes 2752516
  103.4 23.1 %all-to-all-start = ((f32[8,16,8,128]{3,2,1,0:T(8,128)}), f32[8,16,8,128]{3,2,1,0:T(8,128)S(1)}, u32[]{:S(2)}, u32[]{:S(2)}) async-start(f32[8,16,8,128]{3,2,1,0:T(8,128)} %add_add_fusion), calls=%async_computation | async-start | bytes 1048576 | tf_op jit(solution)/shard_map/all_to_all | solution.py:348
  109.1 20.9 %collective-permute-start.9 = (f32[32,3,8,128]{3,2,1,0:T(8,128)S(1)}, f32[32,3,8,128]{3,2,1,0:T(8,128)S(1)}, u32[]{:S(2)}, u32[]{:S(2)}) collective-permute-start(f32[32,3,8,128]{3,2,1,0:T(8,128)S(1)} %slice.17), channel_id=1, source_target_pairs={{0,128},{128,0},{1,129},{129,1},{2,130},{130,2},{3,131},{131,3},{4... | collective-permute-start | bytes 1179656 | tf_op jit(solution)/shard_map/ppermute | solution.py:408
  126.6 0.8 copy-start.2
  130.0 0.8 copy-start.4

commit v2 on v1

--- a/solution.py
+++ b/solution.py
@@ -284,7 +284,7 @@
         for l in range(WIDE):
             x_ref[SUBLANES * d : SUBLANES * (d + 1), block(l)] = mine_ref[d, SLOTS + l]
     total = mine_ref[SUM_PIECE, SUM_SLOT] + other_ref[SUM_PIECE, SUM_SLOT]
-    norm_ref[...] = jnp.sqrt(total / 2048.0)
+    norm_ref[0] = jnp.sqrt(total / 2048.0)[0, 0]
 
     low = {(i, j): w[at(i, j)] for i in range(BLOCKS) for j in range(i + 1)}
     rows = [x_ref[:, block(l)] for l in range(WIDE)]
@@ -307,21 +307,6 @@
             rows[j] = rows[j] - times_transposed(x, low[j, s])
 
 
-def trailing_kernel(place_ref, got_ref, a_ref, out_ref, a_buf, sem):
-    share = out_ref.shape[0]
-    row = pl.multiple_of((place_ref[2] * Y_SIZE + place_ref[3]) * share, share)
-    copy = pltpu.make_async_copy(a_ref.at[pl.ds(row, share)], a_buf, sem)
-    copy.start()
-    copy.wait()
-    for g in range(share // SUBLANES):
-        for l in range(WIDE):
-            total = got_ref[0, g * WIDE + l]
-            for n in range(1, got_ref.shape[0]):
-                total = total + got_ref[n, g * WIDE + l]
-            here = (slice(SUBLANES * g, SUBLANES * (g + 1)), slice(LANES * l, LANES * (l + 1)))
-            out_ref[here] = a_buf[here] - total
-
-
 SMEM = pl.BlockSpec(memory_space=pltpu.SMEM)
 VMEM = pl.BlockSpec(memory_space=pltpu.VMEM)
 ANY = pl.BlockSpec(memory_space=pl.ANY)
@@ -331,8 +316,8 @@
     return jax.ShapeDtypeStruct(dims, F32)
 
 
-def call(kernel, flops, outs, in_specs, scratch=(), grid=(), out_spec=None):
-    out_specs = [out_spec or VMEM] * len(outs)
+def call(kernel, flops, outs, in_specs, scratch=(), grid=(), out_spec=None, out_specs=None):
+    out_specs = out_specs or [out_spec or VMEM] * len(outs)
     return pl.pallas_call(
         kernel,
         out_shape=outs,
@@ -425,22 +410,20 @@
     parts = delivered(parts, Y)
     part = sum(parts)
     got = exchange(part, Z)
-    (trailing,) = call(
-        trailing_kernel,
-        1_000_000_000,
-        [shaped(share, tile_cols)],
-        [SMEM, VMEM, ANY],
-        [pltpu.VMEM((share, tile_cols), F32), pltpu.SemaphoreType.DMA],
-    )(place, got, a_tile)
+    tiles = got.sum(axis=0)
+    tiles = tiles.reshape(4, WIDE, *TILE).transpose(0, 2, 1, 3).reshape(share, tile_cols)
+    d = lax.axis_index(DEPTH)
+    trailing = lax.dynamic_slice_in_dim(a_tile, d * share, share, 0) - tiles
 
     new_panel, norm = call(
         solve_kernel,
         30_000_000_000,
-        [shaped(c_rows, PB), shaped(*TILE)],
+        [shaped(c_rows, PB), shaped(1)],
         [SMEM, VMEM, VMEM],
         [pltpu.VMEM((PAIRS * LANES, LANES), F32)],
+        out_specs=[VMEM, SMEM],
     )(place, mine, other)
-    return (trailing, new_panel, norm[0, :1])
+    return (trailing, new_panel, norm)
 
 
 def solution(mesh):

time: 154 us -> 151 us (0.981)
  Pallas kernels: 42.9 us -> 40.3 us
  local copies, waits for them, and re-layouts: 5.46 us -> 3.5 us
  other arithmetic: 3.38 us -> 4.92 us
    pallas_call x2 -> x1, Pallas kernels: 23.3 us -> 20.7 us  [body(): call(solve_kernel, 30000000000, [shaped(c_rows, PB), shaped(1)], [SMEM, V...]
  transfers between devices with their start and end apart: 13 -> 13, of which waited for: 8 -> 8; matrix products, arithmetic and copies ran while one was open for 2% -> 3% of each run, Pallas kernels for 15% -> 13%
where the time goes in v2:
time: 151 us; the launch traced here: 150 us
  waiting for transfers between devices  63.4 us (42%)
  Pallas kernels  40.3 us (27%)
  starting transfers between devices  36.8 us (24%)
  other arithmetic  4.92 us (3%)
  local copies, waits for them, and re-layouts  3.5 us (2%)
    all_to_all x3, waiting for transfers between devices, exchange(): return lax.all_to_all(pieces, axis, split_axis=0, concat_axis=0, tiled=True)  30.4 us
    ppermute x6, waiting for transfers between devices, shifted(): lax.ppermute(value, axis, [(i, (i + by) % size) for i in range(size)])  30.3 us
    all_to_all x3, starting transfers between devices, exchange(): return lax.all_to_all(pieces, axis, split_axis=0, concat_axis=0, tiled=True)  22.6 us
    pallas_call x1, Pallas kernels, body(): call(solve_kernel, 30000000000, [shaped(c_rows, PB), shaped(1)], [SMEM, V...  20.7 us
    ppermute x6, starting transfers between devices, shifted(): lax.ppermute(value, axis, [(i, (i + by) % size) for i in range(size)])  9.64 us
    pallas_call x1, Pallas kernels, body(): call(block_kernel, 20000000000, [piece] * Y_SIZE, [SMEM, pl.BlockSpec((PB...  8.6 us
    pallas_call x1, Pallas kernels, body(): call(top_kernel, 8000000000, [piece], [SMEM, ANY, ANY], [pltpu.VMEM((c_ro...  6.07 us
    ppermute x1, starting transfers between devices, body(): top = lax.ppermute(panels[:PB], 'row', [(0, 1)])  3.1 us
  transfers between devices with their start and end apart: 13, of which 8 were waited for; matrix products, arithmetic and copies ran while one was open for 3% of the time, Pallas kernels for 13%

profile of v2, /device:TPU:2, one launch (start us, length us, event | category | flops | bytes accessed | tf_op | source)
XLA Modules:
  0.0 149.7 jit_solution(11500222126033847801)
XLA Ops:
  0.6 1.7 %slice.9 = f32[512,1024]{1,0:T(8,128)S(1)} slice(f32[1024,1024]{1,0:T(8,128)} %near_ref.3), slice={[0:512], [0:1024]} | slice | bytes 4194304 | tf_op jit(solution)/shard_map/slice | solution.py:355
  2.4 3.1 %collective-permute-start.4 = (f32[512,1024]{1,0:T(8,128)S(1)}, f32[512,1024]{1,0:T(8,128)}, u32[]{:S(2)}, u32[]{:S(2)}) collective-permute-start(f32[512,1024]{1,0:T(8,128)S(1)} %slice.9), channel_id=1, source_target_pairs={{0,128},{1,129},{2,130},{3,131},{4,132},{5,133},{6,134},{7,135},{8... | collective-permute-start | bytes 6291464 | tf_op jit(solution)/shard_map/ppermute | solution.py:355
  6.1 1.9 %collective-permute-done.4.top_in_ref = f32[512,1024]{1,0:T(8,128)} collective-permute-done((f32[512,1024]{1,0:T(8,128)S(1)}, f32[512,1024]{1,0:T(8,128)}, u32[]{:S(2)}, u32[]{:S(2)}) %collective-permute-start.4) | collective-permute-done | bytes 2097184 | tf_op jit(solution)/shard_map/ppermute | solution.py:355
  8.0 6.1 %shard_map.50 = f32[32,7,8,128]{3,2,1,0:T(8,128)} custom-call(s32[4]{0:T(128)} %pad_add_fusion.place_ref, f32[1024,1024]{1,0:T(8,128)} %near_ref.3, f32[512,1024]{1,0:T(8,128)} %collective-permute-done.4.top_in_ref), custom_call_target="tpu_custom_call" | custom-call | flops 8000000000 | bytes 4000000 | tf_op jit(solution)/shard_map/pallas_call | solution.py:359
  14.1 11.5 %all-to-all-start.1 = ((f32[32,7,8,128]{3,2,1,0:T(8,128)}), f32[32,7,8,128]{3,2,1,0:T(8,128)S(1)}, u32[]{:S(2)}, u32[]{:S(2)}) async-start(f32[32,7,8,128]{3,2,1,0:T(8,128)} %shard_map.50), calls=%async_computation.1 | async-start | bytes 1835008 | tf_op jit(solution)/shard_map/all_to_all | solution.py:333
  25.6 2.6 %shard_map.51 = (f32[11,8,128]{2,1,0:T(8,128)}, f32[11,8,128]{2,1,0:T(8,128)}, f32[11,8,128]{2,1,0:T(8,128)}, f32[11,8,128]{2,1,0:T(8,128)}) custom-call(s32[4]{0:T(128)} %pad_add_fusion.place_ref, f32[1024,512]{1,0:T(8,128)} %a_ref.1), custom_call_target="tpu_custom_call" | custom-call | flops 1000000000 | bytes 4000000 | tf_op jit(solution)/shard_map/pallas_call | solution.py:373
  28.8 2.4 %collective-permute-start.6 = (f32[11,8,128]{2,1,0:T(8,128)}, f32[11,8,128]{2,1,0:T(8,128)S(1)}, u32[]{:S(2)}, u32[]{:S(2)}) collective-permute-start(f32[11,8,128]{2,1,0:T(8,128)} %get-tuple-element.19), channel_id=1, source_target_pairs={{0,64},{32,96},{64,0},{96,32},{1,65},{33,97},{65,1},{97,33},{2,66}... | collective-permute-start | bytes 135176 | tf_op jit(solution)/shard_map/ppermute | solution.py:338
  31.2 1.8 %collective-permute-start.5 = (f32[11,8,128]{2,1,0:T(8,128)}, f32[11,8,128]{2,1,0:T(8,128)S(1)}, u32[]{:S(2)}, u32[]{:S(2)}) collective-permute-start(f32[11,8,128]{2,1,0:T(8,128)} %get-tuple-element.18), channel_id=1, source_target_pairs={{0,32},{32,64},{64,96},{96,0},{1,33},{33,65},{65,97},{97,1},{2,34}... | collective-permute-start | bytes 135176 | tf_op jit(solution)/shard_map/ppermute | solution.py:338
  33.0 1.5 %collective-permute-done.6 = f32[11,8,128]{2,1,0:T(8,128)S(1)} collective-permute-done((f32[11,8,128]{2,1,0:T(8,128)}, f32[11,8,128]{2,1,0:T(8,128)S(1)}, u32[]{:S(2)}, u32[]{:S(2)}) %collective-permute-start.6) | collective-permute-done | bytes 45088 | tf_op jit(solution)/shard_map/ppermute | solution.py:338
  34.6 0.9 collective-permute-done.5
  36.3 1.3 collective-permute-start.8
  38.4 13.0 %all-to-all-done.1.got_ref = f32[32,7,8,128]{3,2,1,0:T(8,128)S(1)} async-done(((f32[32,7,8,128]{3,2,1,0:T(8,128)}), f32[32,7,8,128]{3,2,1,0:T(8,128)S(1)}, u32[]{:S(2)}, u32[]{:S(2)}) %all-to-all-start.1) | async-done | bytes 917536 | tf_op jit(solution)/shard_map/all_to_all | solution.py:333
  51.4 1.0 copy-done.1
  52.4 2.3 %shard_map.52 = f32[32,7,8,128]{3,2,1,0:T(8,128)} custom-call(s32[4]{0:T(128)} %pad_add_fusion.place_ref, f32[32,7,8,128]{3,2,1,0:T(8,128)} %copy-done.1, f32[11,8,128]{2,1,0:T(8,128)} %copy-done.2, f32[3,8,128]{2,1,0:T(8,128)} %copy-done.4), custom_call_target="tpu_custom_call" | custom-call | flops 1000000000 | bytes 4000000 | tf_op jit(solution)/shard_map/pallas_call | solution.py:389
  54.7 5.5 %all-to-all-start.2 = ((f32[32,7,8,128]{3,2,1,0:T(8,128)}), f32[32,7,8,128]{3,2,1,0:T(8,128)S(1)}, u32[]{:S(2)}, u32[]{:S(2)}) async-start(f32[32,7,8,128]{3,2,1,0:T(8,128)} %shard_map.52), calls=%async_computation.2 | async-start | bytes 1835008 | tf_op jit(solution)/shard_map/all_to_all | solution.py:333
  60.2 8.6 %shard_map.49 = (f32[8,16,8,128]{3,2,1,0:T(8,128)}, f32[8,16,8,128]{3,2,1,0:T(8,128)}, f32[8,16,8,128]{3,2,1,0:T(8,128)}, f32[8,16,8,128]{3,2,1,0:T(8,128)}) custom-call(s32[4]{0:T(128)} %pad_add_fusion.place_ref, f32[1024,1024]{1,0:T(8,128)} %near_ref.3, f32[1024,1024]{1,0:T(8,128)} %near_ref.3, f32[1024,1024]{1,0:T(8,128)} %collective-permute-done.far_ref), custom_call_target="tpu_custom_call" | custom-call | flops 20000000000 | bytes 4000000 | tf_op jit(solution)/shard_map/pallas_call | solution.py:396
  68.8 3.1 %collective-permute-start.3 = (f32[8,16,8,128]{3,2,1,0:T(8,128)}, f32[8,16,8,128]{3,2,1,0:T(8,128)S(1)}, u32[]{:S(2)}, u32[]{:S(2)}) collective-permute-start(f32[8,16,8,128]{3,2,1,0:T(8,128)} %get-tuple-element.16), channel_id=1, source_target_pairs={{0,3},{1,0},{2,1},{3,2},{4,7},{5,4},{6,5},{7,6},{8,11},{9,8},{10,9... | collective-permute-start | bytes 1572872 | tf_op jit(solution)/shard_map/ppermute | solution.py:338
  73.7 23.7 %collective-permute-done.3 = f32[8,16,8,128]{3,2,1,0:T(8,128)S(1)} collective-permute-done((f32[8,16,8,128]{3,2,1,0:T(8,128)}, f32[8,16,8,128]{3,2,1,0:T(8,128)S(1)}, u32[]{:S(2)}, u32[]{:S(2)}) %collective-permute-start.3) | collective-permute-done | bytes 524320 | tf_op jit(solution)/shard_map/ppermute | solution.py:338
  97.3 4.2 %collective-permute-done.1 = f32[8,16,8,128]{3,2,1,0:T(8,128)S(1)} collective-permute-done((f32[8,16,8,128]{3,2,1,0:T(8,128)}, f32[8,16,8,128]{3,2,1,0:T(8,128)S(1)}, u32[]{:S(2)}, u32[]{:S(2)}) %collective-permute-start.1) | collective-permute-done | bytes 524320 | tf_op jit(solution)/shard_map/ppermute | solution.py:338
  101.5 1.9 %add_add_fusion = f32[8,16,8,128]{3,2,1,0:T(8,128)} fusion(f32[8,16,8,128]{3,2,1,0:T(8,128)S(1)} %collective-permute-done.3, f32[8,16,8,128]{3,2,1,0:T(8,128)S(1)} %collective-permute-done.2, f32[8,16,8,128]{3,2,1,0:T(8,128)} %get-tuple-element.13, f32[8,16,8,128]{3,2,1,0:T(8,128)S(1)} %collective-permute-done.1), kind=kLoop, calls=%fused_computation | loop fusion | flops 393216 | bytes 2621440 | tf_op jit(solution)/shard_map/add | solution.py:411
  103.4 5.6 %all-to-all-start = ((f32[8,16,8,128]{3,2,1,0:T(8,128)}), f32[8,16,8,128]{3,2,1,0:T(8,128)S(1)}, u32[]{:S(2)}, u32[]{:S(2)}) async-start(f32[8,16,8,128]{3,2,1,0:T(8,128)} %add_add_fusion), calls=%async_computation | async-start | bytes 1048576 | tf_op jit(solution)/shard_map/all_to_all | solution.py:333
  109.2 17.4 %all-to-all-done = f32[8,16,8,128]{3,2,1,0:T(8,128)S(1)} async-done(((f32[8,16,8,128]{3,2,1,0:T(8,128)}), f32[8,16,8,128]{3,2,1,0:T(8,128)S(1)}, u32[]{:S(2)}, u32[]{:S(2)}) %all-to-all-start) | async-done | bytes 524320 | tf_op jit(solution)/shard_map/all_to_all | solution.py:333
  126.6 1.5 dynamic-slice_subtract_fusion
  128.8 20.7 %shard_map.53 = (f32[256,512]{1,0:T(8,128)}, f32[1]{0:T(128)}) custom-call(s32[4]{0:T(128)} %pad_add_fusion.place_ref, f32[32,7,8,128]{3,2,1,0:T(8,128)} %copy-done, f32[32,3,8,128]{3,2,1,0:T(8,128)} %copy-done.3), custom_call_target="tpu_custom_call" | custom-call | flops 30000001024 | bytes 4000000 | tf_op jit(solution)/shard_map/pallas_call | solution.py:418
  (25 shorter events, 5.6 us)
Async XLA Ops:
  2.4 5.6 %collective-permute-start.4 = (f32[512,1024]{1,0:T(8,128)S(1)}, f32[512,1024]{1,0:T(8,128)}, u32[]{:S(2)}, u32[]{:S(2)}) collective-permute-start(f32[512,1024]{1,0:T(8,128)S(1)} %slice.9), channel_id=1, source_target_pairs={{0,128},{1,129},{2,130},{3,131},{4,132},{5,133},{6,134},{7,135},{8... | collective-permute-start | bytes 6291464 | tf_op jit(solution)/shard_map/ppermute | solution.py:355
  5.5 54.8 %collective-permute-start = (f32[1024,1024]{1,0:T(8,128)}, f32[1024,1024]{1,0:T(8,128)}, u32[]{:S(2)}, u32[]{:S(2)}) collective-permute-start(f32[1024,1024]{1,0:T(8,128)} %near_ref.3), channel_id=1, source_target_pairs={{0,128},{128,0},{1,129},{129,1},{2,130},{130,2},{3,131},{131,3},{4... | collective-permute-start | bytes 12582920 | tf_op jit(solution)/shard_map/ppermute | solution.py:356
  14.1 37.3 %all-to-all-start.1 = ((f32[32,7,8,128]{3,2,1,0:T(8,128)}), f32[32,7,8,128]{3,2,1,0:T(8,128)S(1)}, u32[]{:S(2)}, u32[]{:S(2)}) async-start(f32[32,7,8,128]{3,2,1,0:T(8,128)} %shard_map.50), calls=%async_computation.1 | async-start | bytes 1835008 | tf_op jit(solution)/shard_map/all_to_all | solution.py:333
  28.2 4.8 %collective-permute-start.7 = (f32[11,8,128]{2,1,0:T(8,128)}, f32[11,8,128]{2,1,0:T(8,128)S(1)}, u32[]{:S(2)}, u32[]{:S(2)}) collective-permute-start(f32[11,8,128]{2,1,0:T(8,128)} %get-tuple-element.20), channel_id=1, source_target_pairs={{0,96},{32,0},{64,32},{96,64},{1,97},{33,1},{65,33},{97,65},{2,98}... | collective-permute-start | bytes 135176 | tf_op jit(solution)/shard_map/ppermute | solution.py:338
  28.8 5.8 %collective-permute-start.6 = (f32[11,8,128]{2,1,0:T(8,128)}, f32[11,8,128]{2,1,0:T(8,128)S(1)}, u32[]{:S(2)}, u32[]{:S(2)}) collective-permute-start(f32[11,8,128]{2,1,0:T(8,128)} %get-tuple-element.19), channel_id=1, source_target_pairs={{0,64},{32,96},{64,0},{96,32},{1,65},{33,97},{65,1},{97,33},{2,66}... | collective-permute-start | bytes 135176 | tf_op jit(solution)/shard_map/ppermute | solution.py:338
  31.2 4.3 %collective-permute-start.5 = (f32[11,8,128]{2,1,0:T(8,128)}, f32[11,8,128]{2,1,0:T(8,128)S(1)}, u32[]{:S(2)}, u32[]{:S(2)}) collective-permute-start(f32[11,8,128]{2,1,0:T(8,128)} %get-tuple-element.18), channel_id=1, source_target_pairs={{0,32},{32,64},{64,96},{96,0},{1,33},{33,65},{65,97},{97,1},{2,34}... | collective-permute-start | bytes 135176 | tf_op jit(solution)/shard_map/ppermute | solution.py:338
  36.3 15.1 %copy-start.2 = (f32[11,8,128]{2,1,0:T(8,128)}, f32[11,8,128]{2,1,0:T(8,128)S(1)}, u32[]{:S(2)}) copy-start(f32[11,8,128]{2,1,0:T(8,128)S(1)} %add_add_fusion.1.a_ref) | copy-start | bytes 135172
  36.3 2.1 %collective-permute-start.8 = (f32[3,8,128]{2,1,0:T(8,128)S(1)}, f32[3,8,128]{2,1,0:T(8,128)S(1)}, u32[]{:S(2)}, u32[]{:S(2)}) collective-permute-start(f32[3,8,128]{2,1,0:T(8,128)S(1)} %slice.12), channel_id=1, source_target_pairs={{0,128},{1,129},{2,130},{3,131},{4,132},{5,133},{6,134},{7,135},{8... | collective-permute-start | bytes 36872 | tf_op jit(solution)/shard_map/ppermute | solution.py:387
  38.4 13.0 %copy-start.4 = (f32[3,8,128]{2,1,0:T(8,128)}, f32[3,8,128]{2,1,0:T(8,128)S(1)}, u32[]{:S(2)}) copy-start(f32[3,8,128]{2,1,0:T(8,128)S(1)} %collective-permute-done.8.other_ref) | copy-start | bytes 36868
  51.4 1.0 copy-start.1
  54.7 48.8 %all-to-all-start.2 = ((f32[32,7,8,128]{3,2,1,0:T(8,128)}), f32[32,7,8,128]{3,2,1,0:T(8,128)S(1)}, u32[]{:S(2)}, u32[]{:S(2)}) async-start(f32[32,7,8,128]{3,2,1,0:T(8,128)} %shard_map.52), calls=%async_computation.2 | async-start | bytes 1835008 | tf_op jit(solution)/shard_map/all_to_all | solution.py:333
  68.8 28.5 %collective-permute-start.3 = (f32[8,16,8,128]{3,2,1,0:T(8,128)}, f32[8,16,8,128]{3,2,1,0:T(8,128)S(1)}, u32[]{:S(2)}, u32[]{:S(2)}) collective-permute-start(f32[8,16,8,128]{3,2,1,0:T(8,128)} %get-tuple-element.16), channel_id=1, source_target_pairs={{0,3},{1,0},{2,1},{3,2},{4,7},{5,4},{6,5},{7,6},{8,11},{9,8},{10,9... | collective-permute-start | bytes 1572872 | tf_op jit(solution)/shard_map/ppermute | solution.py:338
  71.9 25.4 %collective-permute-start.2 = (f32[8,16,8,128]{3,2,1,0:T(8,128)}, f32[8,16,8,128]{3,2,1,0:T(8,128)S(1)}, u32[]{:S(2)}, u32[]{:S(2)}) collective-permute-start(f32[8,16,8,128]{3,2,1,0:T(8,128)} %get-tuple-element.15), channel_id=1, source_target_pairs={{0,2},{1,3},{2,0},{3,1},{4,6},{5,7},{6,4},{7,5},{8,10},{9,11},{10,... | collective-permute-start | bytes 1572872 | tf_op jit(solution)/shard_map/ppermute | solution.py:338
  72.8 28.7 %collective-permute-start.1 = (f32[8,16,8,128]{3,2,1,0:T(8,128)}, f32[8,16,8,128]{3,2,1,0:T(8,128)S(1)}, u32[]{:S(2)}, u32[]{:S(2)}) collective-permute-start(f32[8,16,8,128]{3,2,1,0:T(8,128)} %get-tuple-element.14), channel_id=1, source_target_pairs={{0,1},{1,2},{2,3},{3,0},{4,5},{5,6},{6,7},{7,4},{8,9},{9,10},{10,1... | collective-permute-start | bytes 1572872 | tf_op jit(solution)/shard_map/ppermute | solution.py:338
  103.4 24.6 %copy-start = (f32[32,7,8,128]{3,2,1,0:T(8,128)}, f32[32,7,8,128]{3,2,1,0:T(8,128)S(1)}, u32[]{:S(2)}) copy-start(f32[32,7,8,128]{3,2,1,0:T(8,128)S(1)} %all-to-all-done.2.mine_ref) | copy-start | bytes 2752516
  103.4 23.1 %all-to-all-start = ((f32[8,16,8,128]{3,2,1,0:T(8,128)}), f32[8,16,8,128]{3,2,1,0:T(8,128)S(1)}, u32[]{:S(2)}, u32[]{:S(2)}) async-start(f32[8,16,8,128]{3,2,1,0:T(8,128)} %add_add_fusion), calls=%async_computation | async-start | bytes 1048576 | tf_op jit(solution)/shard_map/all_to_all | solution.py:333
  109.1 19.0 %collective-permute-start.9 = (f32[32,3,8,128]{3,2,1,0:T(8,128)S(1)}, f32[32,3,8,128]{3,2,1,0:T(8,128)S(1)}, u32[]{:S(2)}, u32[]{:S(2)}) collective-permute-start(f32[32,3,8,128]{3,2,1,0:T(8,128)S(1)} %slice.13), channel_id=1, source_target_pairs={{0,128},{128,0},{1,129},{129,1},{2,130},{130,2},{3,131},{131,3},{4... | collective-permute-start | bytes 1179656 | tf_op jit(solution)/shard_map/ppermute | solution.py:393
  128.1 0.8 copy-start.3

commit v3 on v2

--- a/solution.py
+++ b/solution.py
@@ -40,41 +40,64 @@
 
 
 def inverse_factor(load, store):
-    lane = lax.broadcasted_iota(jnp.int32, (SUBLANES, LANES), 1)
-    sub = lax.broadcasted_iota(jnp.int32, (SUBLANES, LANES), 0)
-    whole = (SUBLANES, LANES)
+    lane = lax.broadcasted_iota(jnp.int32, TILE, 1)
+    sub = lax.broadcasted_iota(jnp.int32, TILE, 0)
+
+    def spread_columns(row, g):
+        first = SUBLANES * g
+        return [
+            jnp.broadcast_to(row[:, first + j : first + j + 1], TILE) for j in range(SUBLANES)
+        ]
+
     rows = [load(h) for h in range(GROUPS)]
+    cols = {(h, 0): spread_columns(rows[h], 0) for h in range(GROUPS)}
+    for h in (1, 2):
+        cols[h, 1] = spread_columns(rows[h], 1)
     for g in range(GROUPS):
         first = SUBLANES * g
-        cols = {
-            h: [
-                jnp.broadcast_to(rows[h][:, first + j : first + j + 1], whole)
-                for j in range(SUBLANES)
-            ]
-            for h in range(g, GROUPS)
-        }
         inside = (lane >= first) & (lane < first + SUBLANES)
-        rows[g] = jnp.where(inside, jnp.where(lane - first == sub, 1.0, 0.0), rows[g])
+        own = cols.pop((g, g))
+        row = jnp.where(inside, jnp.where(lane - first == sub, 1.0, 0.0), rows[g])
+        done = jnp.zeros(TILE, F32)
+        scales, spreads, finals = [], [], []
+        for j in range(SUBLANES):
+            scale = lax.rsqrt(jnp.broadcast_to(own[j][j : j + 1], TILE))
+            final = jnp.broadcast_to(row[j : j + 1], TILE) * scale
+            done = jnp.where(sub == j, final, done)
+            factor = own[j] * scale
+            spread = {k: jnp.broadcast_to(factor[k : k + 1], TILE) for k in range(j + 1, SUBLANES)}
+            for k in spread:
+                own[k] = own[k] - factor * spread[k]
+            row = row - jnp.where(sub > j, factor, 0.0) * final
+            scales.append(scale)
+            spreads.append(spread)
+            finals.append(final)
+        store(g, jnp.where(lane <= first + sub, done, 0.0))
+        ahead = []
         for h in range(g + 1, GROUPS):
-            rows[h] = jnp.where(inside, 0.0, rows[h])
-        done = jnp.zeros(whole, F32)
-        for j in range(SUBLANES):
-            scale = lax.rsqrt(jnp.broadcast_to(cols[g][j][j : j + 1], whole))
-            row = jnp.broadcast_to(rows[g][j : j + 1], whole) * scale
-            done = jnp.where(sub == j, row, done)
-            own = cols[g][j] * scale
-            spread = {
-                k: jnp.broadcast_to(own[k : k + 1], whole) for k in range(j + 1, SUBLANES)
-            }
-            for k in spread:
-                cols[g][k] = cols[g][k] - own * spread[k]
-            rows[g] = rows[g] - jnp.where(sub > j, own, 0.0) * row
-            for h in range(g + 1, GROUPS):
-                below = cols[h][j] * scale
-                rows[h] = rows[h] - below * row
-                for k in spread:
-                    cols[h][k] = cols[h][k] - below * spread[k]
-        store(g, jnp.where(lane <= first + sub, done, 0.0))
+            row = jnp.where(inside, 0.0, rows[h])
+            here = cols.pop((h, g))
+            factors = []
+            for j in range(SUBLANES):
+                factor = here[j] * scales[j]
+                for k in spreads[j]:
+                    here[k] = here[k] - factor * spreads[j][k]
+                row = row - factor * finals[j]
+                factors.append(factor)
+            rows[h] = row
+            if h == g + 1:
+                ahead = [
+                    [jnp.broadcast_to(f[k : k + 1], TILE) for k in range(SUBLANES)] for f in factors
+                ]
+            if h <= g + 2:
+                late = cols[h, g + 1]
+                for j in range(SUBLANES):
+                    for k in range(SUBLANES):
+                        late[k] = late[k] - factors[j] * ahead[j][k]
+            else:
+                cols[h, g + 1] = spread_columns(row, g + 1)
+            if g + 2 <= h <= g + 3:
+                cols[h, g + 2] = spread_columns(row, g + 2)
 
 
 def halves(value):
@@ -89,7 +112,7 @@
     return dot(left[0], right[0]) + (dot(left[0], right[1]) + dot(left[1], right[0]))
 
 
-def top_kernel(place_ref, near_ref, top_in_ref, out_ref, own_ref, top_ref, all_ref, sem):
+def top_kernel(place_ref, near_ref, top_in_ref, hbm_ref, own_ref, top_ref, all_ref, out_ref, sem):
     r, c = place_ref[0], place_ref[1]
     count = own_ref.shape[0]
     first = pl.multiple_of(c * count, count)
@@ -115,6 +138,9 @@
             out_ref[d, SLOTS + l] = value[
                 SUBLANES * d : SUBLANES * (d + 1), LANES * l : LANES * (l + 1)
             ]
+    panel = pl.ds(SLOTS, WIDE)
+    panel = pltpu.make_async_copy(out_ref.at[:, panel], hbm_ref.at[:, panel], sem.at[3])
+    panel.start()
     for half in range(2):
 
         @pl.when(r == half)
@@ -149,6 +175,11 @@
     for a in range(SUBLANES):
         tile = jnp.where(sub == a, sums[:, LANES * a : LANES * (a + 1)], tile)
     out_ref[SUM_PIECE, SUM_SLOT] = tile
+    square = pl.ds(0, SLOTS)
+    square = pltpu.make_async_copy(out_ref.at[:, square], hbm_ref.at[:, square], sem.at[4])
+    square.start()
+    panel.wait()
+    square.wait()
 
 
 def a_kernel(place_ref, a_ref, *refs):
@@ -200,26 +231,45 @@
         outs[s][2 * SLOTS + WIDE] = diagonal
 
 
-def merge_kernel(place_ref, got_ref, a_ref, other_ref, out_ref):
+def merge_kernel(place_ref, got_ref, a_ref, other_ref, out_ref, got_buf, a_buf, other_buf, piece, sem):
     r, d = place_ref[0], place_ref[2] * Y_SIZE + place_ref[3]
-    total = got_ref[0]
-    for n in range(1, got_ref.shape[0]):
-        total = total + got_ref[n]
-    tiles = []
+    count = got_ref.shape[0]
+    chunk = count // 4
+    loads = [
+        pltpu.make_async_copy(
+            got_ref.at[pl.ds(chunk * n, chunk)], got_buf.at[pl.ds(chunk * n, chunk)], sem.at[n]
+        )
+        for n in range(4)
+    ]
+    loads.append(pltpu.make_async_copy(a_ref, a_buf, sem.at[4]))
+    loads.append(pltpu.make_async_copy(other_ref, other_buf, sem.at[5]))
+    for load in loads:
+        load.start()
+    total = [jnp.zeros(TILE, F32)] * (SLOTS + WIDE)
+    for n in range(4):
+        loads[n].wait()
+        for m in range(chunk * n, chunk * (n + 1)):
+            total = [t + got_buf[m, k] for k, t in enumerate(total)]
+    loads[4].wait()
+    loads[5].wait()
     for k in range(SLOTS):
-        a = jnp.where(r == 0, a_ref[k], other_ref[k])
+        a = jnp.where(r == 0, a_buf[k], other_buf[k])
         if k == SUM_SLOT:
             special = d == SUM_PIECE
-            value = jnp.where(special, a_ref[2 * SLOTS + WIDE], a) - total[k]
+            value = jnp.where(special, a_buf[2 * SLOTS + WIDE], a) - total[k]
             squares = jnp.sum(jnp.sum(value * value, axis=1, keepdims=True), axis=0, keepdims=True)
-            tiles.append(jnp.where(special, jnp.broadcast_to(squares, TILE), value))
+            piece[k] = jnp.where(special, jnp.broadcast_to(squares, TILE), value)
         else:
-            tiles.append(a - total[k])
+            piece[k] = a - total[k]
     for l in range(WIDE):
-        tiles.append(a_ref[2 * SLOTS + l] - total[SLOTS + l])
-    for n in range(out_ref.shape[0]):
-        for k, tile in enumerate(tiles):
-            out_ref[n, k] = tile
+        piece[SLOTS + l] = a_buf[2 * SLOTS + l] - total[SLOTS + l]
+    stores = [
+        pltpu.make_async_copy(piece, out_ref.at[n], sem.at[6 + n]) for n in range(out_ref.shape[0])
+    ]
+    for store in stores:
+        store.start()
+    for store in stores:
+        store.wait()
 
 
 def block_kernel(place_ref, left_ref, near_ref, far_ref, *refs):
@@ -267,8 +317,17 @@
     return slice(LANES * i, LANES * (i + 1))
 
 
-def solve_kernel(place_ref, mine_ref, other_ref, x_ref, norm_ref, w):
+def solve_kernel(place_ref, mine_in_ref, other_in_ref, x_ref, norm_ref, other_ref, mine_ref, w, sem):
     r = place_ref[0]
+    load = pltpu.make_async_copy(other_in_ref.at[:, pl.ds(0, SLOTS)], other_ref, sem.at[0])
+    load.start()
+    own = pltpu.make_async_copy(mine_in_ref, mine_ref, sem.at[1])
+    own.start()
+    own.wait()
+    for d in range(mine_ref.shape[0]):
+        for l in range(WIDE):
+            x_ref[SUBLANES * d : SUBLANES * (d + 1), block(l)] = mine_ref[d, SLOTS + l]
+    load.wait()
     for half in range(2):
         for ref, take in ((mine_ref, r == half), (other_ref, r != half)):
 
@@ -280,9 +339,6 @@
                         row = LANES * pair(i, j) + SUBLANES * h
                         w[row : row + SUBLANES] = ref[d, k]
 
-    for d in range(mine_ref.shape[0]):
-        for l in range(WIDE):
-            x_ref[SUBLANES * d : SUBLANES * (d + 1), block(l)] = mine_ref[d, SLOTS + l]
     total = mine_ref[SUM_PIECE, SUM_SLOT] + other_ref[SUM_PIECE, SUM_SLOT]
     norm_ref[0] = jnp.sqrt(total / 2048.0)[0, 0]
 
@@ -316,7 +372,7 @@
     return jax.ShapeDtypeStruct(dims, F32)
 
 
-def call(kernel, flops, outs, in_specs, scratch=(), grid=(), out_spec=None, out_specs=None):
+def call(kernel, flops, outs, in_specs, scratch=(), grid=(), out_spec=None, out_specs=None, room=None):
     out_specs = out_specs or [out_spec or VMEM] * len(outs)
     return pl.pallas_call(
         kernel,
@@ -325,6 +381,7 @@
         in_specs=in_specs,
         out_specs=out_specs,
         scratch_shapes=scratch,
+        compiler_params=pltpu.CompilerParams(vmem_limit_bytes=room),
         cost_estimate=pl.CostEstimate(flops=flops, bytes_accessed=4_000_000, transcendentals=0),
     )
 
@@ -365,8 +422,11 @@
             pltpu.VMEM((c_rows, k_size), F32),
             pltpu.VMEM((PB, k_size), F32),
             pltpu.VMEM((tile_rows, k_size), F32),
-            pltpu.SemaphoreType.DMA((3,)),
+            pltpu.VMEM(piece.shape, F32),
+            pltpu.SemaphoreType.DMA((5,)),
         ],
+        out_specs=[ANY],
+        room=32 << 20,
     )(place, panels, top)
     got = exchange(part, DEPTH)
 
@@ -387,10 +447,22 @@
     a_other = lax.ppermute(a_got[SLOTS : 2 * SLOTS], "row", [(0, 1)])
 
     (piece_copies,) = call(
-        merge_kernel, 1_000_000_000, [piece], [SMEM, VMEM, VMEM, VMEM]
+        merge_kernel,
+        1_000_000_000,
+        [piece],
+        [SMEM, ANY, ANY, ANY],
+        [
+            pltpu.VMEM(piece.shape, F32),
+            pltpu.VMEM(a_got.shape, F32),
+            pltpu.VMEM(a_other.shape, F32),
+            pltpu.VMEM(piece.shape[1:], F32),
+            pltpu.SemaphoreType.DMA((6 + depth,)),
+        ],
+        out_specs=[ANY],
+        room=8 << 20,
     )(place, got, a_got, a_other)
     mine = exchange(piece_copies, DEPTH)
-    other = lax.ppermute(mine[:, :SLOTS], "row", swap)
+    other = lax.ppermute(mine, "row", swap)
 
     piece = shaped(z_size, 4 * WIDE, *TILE)
     parts = call(
@@ -406,6 +478,7 @@
         ],
         grid=(2,),
         out_spec=pl.BlockSpec((z_size // 2, *piece.shape[1:]), lambda i: (i, 0, 0, 0)),
+        room=32 << 20,
     )(place, panels, panels, far)
     parts = delivered(parts, Y)
     part = sum(parts)
@@ -419,9 +492,15 @@
         solve_kernel,
         30_000_000_000,
         [shaped(c_rows, PB), shaped(1)],
-        [SMEM, VMEM, VMEM],
-        [pltpu.VMEM((PAIRS * LANES, LANES), F32)],
+        [SMEM, ANY, ANY],
+        [
+            pltpu.VMEM((depth, SLOTS, *TILE), F32),
+            pltpu.VMEM(mine.shape, F32),
+            pltpu.VMEM((PAIRS * LANES, LANES), F32),
+            pltpu.SemaphoreType.DMA((2,)),
+        ],
         out_specs=[VMEM, SMEM],
+        room=24 << 20,
     )(place, mine, other)
     return (trailing, new_panel, norm)
 

time: 151 us -> 144 us (0.954)
  Pallas kernels: 40.3 us -> 35 us
  starting transfers between devices: 36.8 us -> 34.9 us
  waiting for transfers between devices: 63.4 us -> 65.1 us
  other arithmetic: 4.92 us -> 3.3 us
    pallas_call x2, Pallas kernels: 23 us -> 18.9 us  [the longest x1 15.7 us: body(): call(solve_kernel, 30000000000, [shaped(c_rows, PB), shaped(1)], [SMEM, A...]
    ppermute x1, waiting for transfers between devices: 1.88 us -> 3.65 us  [body(): top = lax.ppermute(panels[:PB], 'row', [(0, 1)])]
    unnamed x10 -> x4, local copies, waits for them, and re-layouts: 1.74 us -> 0.01 us
  transfers between devices with their start and end apart: 13 -> 13, of which waited for: 8 -> 9; matrix products, arithmetic and copies ran while one was open for 3% -> 2% of each run, Pallas kernels for 13% -> 14%
where the time goes in v3:
time: 144 us; the launch traced here: 142 us
  waiting for transfers between devices  65.1 us (45%)
  Pallas kernels  35 us (24%)
  starting transfers between devices  34.9 us (24%)
  other arithmetic  3.3 us (2%)
  local copies, waits for them, and re-layouts  3.22 us (2%)
    ppermute x6, waiting for transfers between devices, shifted(): lax.ppermute(value, axis, [(i, (i + by) % size) for i in range(size)])  30.7 us
    all_to_all x3, waiting for transfers between devices, exchange(): return lax.all_to_all(pieces, axis, split_axis=0, concat_axis=0, tiled=True)  29.8 us
    all_to_all x3, starting transfers between devices, exchange(): return lax.all_to_all(pieces, axis, split_axis=0, concat_axis=0, tiled=True)  22 us
    pallas_call x1, Pallas kernels, body(): call(solve_kernel, 30000000000, [shaped(c_rows, PB), shaped(1)], [SMEM, A...  15.7 us
    ppermute x6, starting transfers between devices, shifted(): lax.ppermute(value, axis, [(i, (i + by) % size) for i in range(size)])  9.63 us
    pallas_call x1, Pallas kernels, body(): call(block_kernel, 20000000000, [piece] * Y_SIZE, [SMEM, pl.BlockSpec((PB...  7.62 us
    pallas_call x1, Pallas kernels, body(): call(top_kernel, 8000000000, [piece], [SMEM, ANY, ANY], [pltpu.VMEM((c_ro...  5.78 us
    ppermute x1, waiting for transfers between devices, body(): top = lax.ppermute(panels[:PB], 'row', [(0, 1)])  3.65 us
  transfers between devices with their start and end apart: 13, of which 9 were waited for; matrix products, arithmetic and copies ran while one was open for 2% of the time, Pallas kernels for 14%

profile of v3, /device:TPU:2, one launch (start us, length us, event | category | flops | bytes accessed | tf_op | source)
XLA Modules:
  0.0 142.3 jit_solution(15184715835891894828)
XLA Ops:
  0.6 3.2 %slice.6 = f32[512,1024]{1,0:T(8,128)} slice(f32[1024,1024]{1,0:T(8,128)} %near_ref.3), slice={[0:512], [0:1024]} | slice | bytes 4194304 | tf_op jit(solution)/shard_map/slice | solution.py:412
  3.8 1.9 %collective-permute-start.4 = (f32[512,1024]{1,0:T(8,128)}, f32[512,1024]{1,0:T(8,128)S(1)}, u32[]{:S(2)}, u32[]{:S(2)}) collective-permute-start(f32[512,1024]{1,0:T(8,128)} %slice.6), channel_id=1, source_target_pairs={{0,128},{1,129},{2,130},{3,131},{4,132},{5,133},{6,134},{7,135},{8... | collective-permute-start | bytes 6291464 | tf_op jit(solution)/shard_map/ppermute | solution.py:412
  5.9 3.7 %collective-permute-done.4.top_in_ref = f32[512,1024]{1,0:T(8,128)S(1)} collective-permute-done((f32[512,1024]{1,0:T(8,128)}, f32[512,1024]{1,0:T(8,128)S(1)}, u32[]{:S(2)}, u32[]{:S(2)}) %collective-permute-start.4) | collective-permute-done | bytes 2097184 | tf_op jit(solution)/shard_map/ppermute | solution.py:412
  9.5 5.8 %shard_map.50 = f32[32,7,8,128]{3,2,1,0:T(8,128)} custom-call(s32[4]{0:T(128)S(1)} %pad_add_fusion.place_ref, f32[1024,1024]{1,0:T(8,128)} %near_ref.3, f32[512,1024]{1,0:T(8,128)S(1)} %collective-permute-done.4.top_in_ref), custom_call_target="tpu_custom_call" | custom-call | flops 8000000000 | bytes 4000000 | tf_op jit(solution)/shard_map/pallas_call | solution.py:416
  15.3 11.5 %all-to-all-start.1 = ((f32[32,7,8,128]{3,2,1,0:T(8,128)}), f32[32,7,8,128]{3,2,1,0:T(8,128)S(1)}, u32[]{:S(2)}, u32[]{:S(2)}) async-start(f32[32,7,8,128]{3,2,1,0:T(8,128)} %shard_map.50), calls=%async_computation.1 | async-start | bytes 1835008 | tf_op jit(solution)/shard_map/all_to_all | solution.py:390
  26.9 2.7 %shard_map.51 = (f32[11,8,128]{2,1,0:T(8,128)}, f32[11,8,128]{2,1,0:T(8,128)}, f32[11,8,128]{2,1,0:T(8,128)}, f32[11,8,128]{2,1,0:T(8,128)}) custom-call(s32[4]{0:T(128)} %copy-done, f32[1024,512]{1,0:T(8,128)} %a_ref.1), custom_call_target="tpu_custom_call" | custom-call | flops 1000000000 | bytes 4000000 | tf_op jit(solution)/shard_map/pallas_call | solution.py:433
  30.2 2.4 %collective-permute-start.6 = (f32[11,8,128]{2,1,0:T(8,128)}, f32[11,8,128]{2,1,0:T(8,128)S(1)}, u32[]{:S(2)}, u32[]{:S(2)}) collective-permute-start(f32[11,8,128]{2,1,0:T(8,128)} %get-tuple-element.19), channel_id=1, source_target_pairs={{0,64},{32,96},{64,0},{96,32},{1,65},{33,97},{65,1},{97,33},{2,66}... | collective-permute-start | bytes 135176 | tf_op jit(solution)/shard_map/ppermute | solution.py:395
  32.6 1.8 %collective-permute-start.5 = (f32[11,8,128]{2,1,0:T(8,128)}, f32[11,8,128]{2,1,0:T(8,128)S(1)}, u32[]{:S(2)}, u32[]{:S(2)}) collective-permute-start(f32[11,8,128]{2,1,0:T(8,128)} %get-tuple-element.18), channel_id=1, source_target_pairs={{0,32},{32,64},{64,96},{96,0},{1,33},{33,65},{65,97},{97,1},{2,34}... | collective-permute-start | bytes 135176 | tf_op jit(solution)/shard_map/ppermute | solution.py:395
  34.4 1.5 %collective-permute-done.6 = f32[11,8,128]{2,1,0:T(8,128)S(1)} collective-permute-done((f32[11,8,128]{2,1,0:T(8,128)}, f32[11,8,128]{2,1,0:T(8,128)S(1)}, u32[]{:S(2)}, u32[]{:S(2)}) %collective-permute-start.6) | collective-permute-done | bytes 45088 | tf_op jit(solution)/shard_map/ppermute | solution.py:395
  35.9 0.9 collective-permute-done.5
  37.6 1.3 collective-permute-start.8
  39.8 12.4 %all-to-all-done.1.got_ref = f32[32,7,8,128]{3,2,1,0:T(8,128)S(1)} async-done(((f32[32,7,8,128]{3,2,1,0:T(8,128)}), f32[32,7,8,128]{3,2,1,0:T(8,128)S(1)}, u32[]{:S(2)}, u32[]{:S(2)}) %all-to-all-start.1) | async-done | bytes 917536 | tf_op jit(solution)/shard_map/all_to_all | solution.py:390
  52.1 3.2 %shard_map.52 = f32[32,7,8,128]{3,2,1,0:T(8,128)} custom-call(s32[4]{0:T(128)S(1)} %copy-done.1, f32[32,7,8,128]{3,2,1,0:T(8,128)S(1)} %all-to-all-done.1.got_ref, f32[11,8,128]{2,1,0:T(8,128)S(1)} %add_add_fusion.1.a_ref, f32[3,8,128]{2,1,0:T(8,128)S(1)} %collective-permute-done.8.other_ref), custom_call_target="tpu_custom_call" | custom-call | flops 1000000000 | bytes 4000000 | tf_op jit(solution)/shard_map/pallas_call | solution.py:449
  55.3 5.4 %all-to-all-start.2 = ((f32[32,7,8,128]{3,2,1,0:T(8,128)}), f32[32,7,8,128]{3,2,1,0:T(8,128)S(1)}, u32[]{:S(2)}, u32[]{:S(2)}) async-start(f32[32,7,8,128]{3,2,1,0:T(8,128)} %shard_map.52), calls=%async_computation.2 | async-start | bytes 1835008 | tf_op jit(solution)/shard_map/all_to_all | solution.py:390
  60.8 7.6 %shard_map.49 = (f32[8,16,8,128]{3,2,1,0:T(8,128)S(1)}, f32[8,16,8,128]{3,2,1,0:T(8,128)S(1)}, f32[8,16,8,128]{3,2,1,0:T(8,128)S(1)}, f32[8,16,8,128]{3,2,1,0:T(8,128)S(1)}) custom-call(s32[4]{0:T(128)S(1)} %copy-done.1, f32[1024,1024]{1,0:T(8,128)} %near_ref.3, f32[1024,1024]{1,0:T(8,128)} %near_ref.3, f32[1024,1024]{1,0:T(8,128)} %collective-permute-done.far_ref), custom_call_target="tpu_custom_call" | custom-call | flops 20000000000 | bytes 4000000 | tf_op jit(solution)/shard_map/pallas_call | solution.py:468
  68.4 3.1 %collective-permute-start.3 = (f32[8,16,8,128]{3,2,1,0:T(8,128)S(1)}, f32[8,16,8,128]{3,2,1,0:T(8,128)S(1)}, u32[]{:S(2)}, u32[]{:S(2)}) collective-permute-start(f32[8,16,8,128]{3,2,1,0:T(8,128)S(1)} %get-tuple-element.16), channel_id=1, source_target_pairs={{0,3},{1,0},{2,1},{3,2},{4,7},{5,4},{6,5},{7,6},{8,11},{9,8},{10,9... | collective-permute-start | bytes 1572872 | tf_op jit(solution)/shard_map/ppermute | solution.py:395
  73.2 14.6 %collective-permute-done.3 = f32[8,16,8,128]{3,2,1,0:T(8,128)S(1)} collective-permute-done((f32[8,16,8,128]{3,2,1,0:T(8,128)S(1)}, f32[8,16,8,128]{3,2,1,0:T(8,128)S(1)}, u32[]{:S(2)}, u32[]{:S(2)}) %collective-permute-start.3) | collective-permute-done | bytes 524320 | tf_op jit(solution)/shard_map/ppermute | solution.py:395
  87.8 3.7 %collective-permute-done.2 = f32[8,16,8,128]{3,2,1,0:T(8,128)S(1)} collective-permute-done((f32[8,16,8,128]{3,2,1,0:T(8,128)S(1)}, f32[8,16,8,128]{3,2,1,0:T(8,128)S(1)}, u32[]{:S(2)}, u32[]{:S(2)}) %collective-permute-start.2) | collective-permute-done | bytes 524320 | tf_op jit(solution)/shard_map/ppermute | solution.py:395
  91.5 10.0 %collective-permute-done.1 = f32[8,16,8,128]{3,2,1,0:T(8,128)S(1)} collective-permute-done((f32[8,16,8,128]{3,2,1,0:T(8,128)S(1)}, f32[8,16,8,128]{3,2,1,0:T(8,128)S(1)}, u32[]{:S(2)}, u32[]{:S(2)}) %collective-permute-start.1) | collective-permute-done | bytes 524320 | tf_op jit(solution)/shard_map/ppermute | solution.py:395
  101.5 0.9 add_add_fusion
  102.4 5.1 %all-to-all-start = ((f32[8,16,8,128]{3,2,1,0:T(8,128)}), f32[8,16,8,128]{3,2,1,0:T(8,128)S(1)}, u32[]{:S(2)}, u32[]{:S(2)}) async-start(f32[8,16,8,128]{3,2,1,0:T(8,128)} %add_add_fusion), calls=%async_computation | async-start | bytes 1048576 | tf_op jit(solution)/shard_map/all_to_all | solution.py:390
  107.5 17.5 %all-to-all-done = f32[8,16,8,128]{3,2,1,0:T(8,128)S(1)} async-done(((f32[8,16,8,128]{3,2,1,0:T(8,128)}), f32[8,16,8,128]{3,2,1,0:T(8,128)S(1)}, u32[]{:S(2)}, u32[]{:S(2)}) %all-to-all-start) | async-done | bytes 524320 | tf_op jit(solution)/shard_map/all_to_all | solution.py:390
  125.0 1.5 %dynamic-slice_subtract_fusion = f32[32,512]{1,0:T(8,128)} fusion(f32[32,512]{1,0:T(8,128)S(1)} %bitcast.9, f32[1024,512]{1,0:T(8,128)} %a_ref.1, s32[]{:T(128)S(6)} %select_n.3), kind=kLoop, calls=%fused_computation.1 | loop fusion | flops 16384 | bytes 196612 | tf_op jit(solution)/shard_map/sub | solution.py:489
  126.5 15.7 %shard_map.53 = (f32[256,512]{1,0:T(8,128)}, f32[1]{0:T(128)}) custom-call(s32[4]{0:T(128)S(1)} %copy-done.1, f32[32,7,8,128]{3,2,1,0:T(8,128)S(1)} %all-to-all-done.2.mine_in_ref, f32[32,7,8,128]{3,2,1,0:T(8,128)S(1)} %collective-permute-done.9.other_in_ref), custom_call_target="tpu_custom_call" | custom-call | flops 30000001024 | bytes 4000000 | tf_op jit(solution)/shard_map/pallas_call | solution.py:491
  (18 shorter events, 4.2 us)
Async XLA Ops:
  3.8 5.7 %collective-permute-start.4 = (f32[512,1024]{1,0:T(8,128)}, f32[512,1024]{1,0:T(8,128)S(1)}, u32[]{:S(2)}, u32[]{:S(2)}) collective-permute-start(f32[512,1024]{1,0:T(8,128)} %slice.6), channel_id=1, source_target_pairs={{0,128},{1,129},{2,130},{3,131},{4,132},{5,133},{6,134},{7,135},{8... | collective-permute-start | bytes 6291464 | tf_op jit(solution)/shard_map/ppermute | solution.py:412
  5.7 55.1 %collective-permute-start = (f32[1024,1024]{1,0:T(8,128)}, f32[1024,1024]{1,0:T(8,128)}, u32[]{:S(2)}, u32[]{:S(2)}) collective-permute-start(f32[1024,1024]{1,0:T(8,128)} %near_ref.3), channel_id=1, source_target_pairs={{0,128},{128,0},{1,129},{129,1},{2,130},{130,2},{3,131},{131,3},{4... | collective-permute-start | bytes 12582920 | tf_op jit(solution)/shard_map/ppermute | solution.py:413
  5.9 9.4 %copy-start = (s32[4]{0:T(128)}, s32[4]{0:T(128)S(1)}, u32[]{:S(2)}) copy-start(s32[4]{0:T(128)S(1)} %pad_add_fusion.place_ref) | copy-start | bytes 52
  15.3 36.8 %all-to-all-start.1 = ((f32[32,7,8,128]{3,2,1,0:T(8,128)}), f32[32,7,8,128]{3,2,1,0:T(8,128)S(1)}, u32[]{:S(2)}, u32[]{:S(2)}) async-start(f32[32,7,8,128]{3,2,1,0:T(8,128)} %shard_map.50), calls=%async_computation.1 | async-start | bytes 1835008 | tf_op jit(solution)/shard_map/all_to_all | solution.py:390
  26.9 25.3 %copy-start.1 = (s32[4]{0:T(128)S(1)}, s32[4]{0:T(128)}, u32[]{:S(2)}) copy-start(s32[4]{0:T(128)} %copy-done) | copy-start | bytes 52
  29.5 4.8 %collective-permute-start.7 = (f32[11,8,128]{2,1,0:T(8,128)}, f32[11,8,128]{2,1,0:T(8,128)S(1)}, u32[]{:S(2)}, u32[]{:S(2)}) collective-permute-start(f32[11,8,128]{2,1,0:T(8,128)} %get-tuple-element.20), channel_id=1, source_target_pairs={{0,96},{32,0},{64,32},{96,64},{1,97},{33,1},{65,33},{97,65},{2,98}... | collective-permute-start | bytes 135176 | tf_op jit(solution)/shard_map/ppermute | solution.py:395
  30.2 5.8 %collective-permute-start.6 = (f32[11,8,128]{2,1,0:T(8,128)}, f32[11,8,128]{2,1,0:T(8,128)S(1)}, u32[]{:S(2)}, u32[]{:S(2)}) collective-permute-start(f32[11,8,128]{2,1,0:T(8,128)} %get-tuple-element.19), channel_id=1, source_target_pairs={{0,64},{32,96},{64,0},{96,32},{1,65},{33,97},{65,1},{97,33},{2,66}... | collective-permute-start | bytes 135176 | tf_op jit(solution)/shard_map/ppermute | solution.py:395
  32.6 4.3 %collective-permute-start.5 = (f32[11,8,128]{2,1,0:T(8,128)}, f32[11,8,128]{2,1,0:T(8,128)S(1)}, u32[]{:S(2)}, u32[]{:S(2)}) collective-permute-start(f32[11,8,128]{2,1,0:T(8,128)} %get-tuple-element.18), channel_id=1, source_target_pairs={{0,32},{32,64},{64,96},{96,0},{1,33},{33,65},{65,97},{97,1},{2,34}... | collective-permute-start | bytes 135176 | tf_op jit(solution)/shard_map/ppermute | solution.py:395
  37.6 2.1 %collective-permute-start.8 = (f32[3,8,128]{2,1,0:T(8,128)S(1)}, f32[3,8,128]{2,1,0:T(8,128)S(1)}, u32[]{:S(2)}, u32[]{:S(2)}) collective-permute-start(f32[3,8,128]{2,1,0:T(8,128)S(1)} %slice.8), channel_id=1, source_target_pairs={{0,128},{1,129},{2,130},{3,131},{4,132},{5,133},{6,134},{7,135},{8... | collective-permute-start | bytes 36872 | tf_op jit(solution)/shard_map/ppermute | solution.py:447
  55.3 47.1 %all-to-all-start.2 = ((f32[32,7,8,128]{3,2,1,0:T(8,128)}), f32[32,7,8,128]{3,2,1,0:T(8,128)S(1)}, u32[]{:S(2)}, u32[]{:S(2)}) async-start(f32[32,7,8,128]{3,2,1,0:T(8,128)} %shard_map.52), calls=%async_computation.2 | async-start | bytes 1835008 | tf_op jit(solution)/shard_map/all_to_all | solution.py:390
  68.4 19.4 %collective-permute-start.3 = (f32[8,16,8,128]{3,2,1,0:T(8,128)S(1)}, f32[8,16,8,128]{3,2,1,0:T(8,128)S(1)}, u32[]{:S(2)}, u32[]{:S(2)}) collective-permute-start(f32[8,16,8,128]{3,2,1,0:T(8,128)S(1)} %get-tuple-element.16), channel_id=1, source_target_pairs={{0,3},{1,0},{2,1},{3,2},{4,7},{5,4},{6,5},{7,6},{8,11},{9,8},{10,9... | collective-permute-start | bytes 1572872 | tf_op jit(solution)/shard_map/ppermute | solution.py:395
  71.5 20.0 %collective-permute-start.2 = (f32[8,16,8,128]{3,2,1,0:T(8,128)S(1)}, f32[8,16,8,128]{3,2,1,0:T(8,128)S(1)}, u32[]{:S(2)}, u32[]{:S(2)}) collective-permute-start(f32[8,16,8,128]{3,2,1,0:T(8,128)S(1)} %get-tuple-element.15), channel_id=1, source_target_pairs={{0,2},{1,3},{2,0},{3,1},{4,6},{5,7},{6,4},{7,5},{8,10},{9,11},{10,... | collective-permute-start | bytes 1572872 | tf_op jit(solution)/shard_map/ppermute | solution.py:395
  72.4 29.1 %collective-permute-start.1 = (f32[8,16,8,128]{3,2,1,0:T(8,128)S(1)}, f32[8,16,8,128]{3,2,1,0:T(8,128)S(1)}, u32[]{:S(2)}, u32[]{:S(2)}) collective-permute-start(f32[8,16,8,128]{3,2,1,0:T(8,128)S(1)} %get-tuple-element.14), channel_id=1, source_target_pairs={{0,1},{1,2},{2,3},{3,0},{4,5},{5,6},{6,7},{7,4},{8,9},{9,10},{10,1... | collective-permute-start | bytes 1572872 | tf_op jit(solution)/shard_map/ppermute | solution.py:395
  102.4 22.6 %all-to-all-start = ((f32[8,16,8,128]{3,2,1,0:T(8,128)}), f32[8,16,8,128]{3,2,1,0:T(8,128)S(1)}, u32[]{:S(2)}, u32[]{:S(2)}) async-start(f32[8,16,8,128]{3,2,1,0:T(8,128)} %add_add_fusion), calls=%async_computation | async-start | bytes 1048576 | tf_op jit(solution)/shard_map/all_to_all | solution.py:390
  107.5 19.0 %collective-permute-start.9 = (f32[32,7,8,128]{3,2,1,0:T(8,128)S(1)}, f32[32,7,8,128]{3,2,1,0:T(8,128)S(1)}, u32[]{:S(2)}, u32[]{:S(2)}) collective-permute-start(f32[32,7,8,128]{3,2,1,0:T(8,128)S(1)} %all-to-all-done.2.mine_in_ref), channel_id=1, source_target_pairs={{0,128},{128,0},{1,129},{129,1},{2,130},{130,2},{3,131},{131,3},{4... | collective-permute-start | bytes 2752520 | tf_op jit(solution)/shard_map/ppermute | solution.py:465
